TPU v7x, 32 devices: a whole 2x2x4 slice. The times are simulated.
32 devices in a mesh: row: 4 (over z), col: 4 (over y, x), layer: 2 (over core).
Axes of the slice: x: 2, y: 2, z: 4, core: 2. Of those that a mesh axis runs over, the one named last changes fastest.
Arguments:
- matrix: float32 [16, 512, 16, 512], P('row', None, 'col', 'layer'), may hold values from -40 to 40, as said below
- transforms: float32 [1, 8, 1024, 1024], P(None, 'row', ('col', 'layer')), may hold values from -0.1875 to 0.1875
Outputs:
- swept: float32 [16, 512, 16, 512], P('row', None, 'col', 'layer')
Inputs may be any that keep to these rules, and one draw needn't show every extreme that they name: `matrix`: symmetric: entry [i, a, j, b] equals entry [j, b, i, a].
All inputs are finite; a program needn't handle non-finite values.
Results may differ from a plain program's by a relative error of at most 0.0001.
Values sent between devices are 32-bit elements; how exact they have to be, the bound alone decides.
A program may use at most 192 MiB of HBM per device.

v0:
```python
import functools

import jax
import jax.numpy as jnp
from jax import lax
from jax.experimental import pallas as pl
from jax.experimental.pallas import tpu as pltpu
from jax.sharding import PartitionSpec as P

MESH = pl.DeviceIdType.MESH
LANES = 128
ROWS = 128
VMEM_LIMIT = 66_000_000


def halves_of(x):
    high = x.astype(jnp.bfloat16)
    low = (x - high.astype(jnp.float32)).astype(jnp.bfloat16)
    return high, low


def three_dots(a_high, a_low, b_high, b_low):
    def dot(a, b):
        return lax.dot_general(a, b, (((1,), (0,)), ((), ())), preferred_element_type=jnp.float32)

    return dot(a_high, b_high) + (dot(a_high, b_low) + dot(a_low, b_high))


def sweep(
    size,
    a_ref, t_ref,
    out_ref, ap_ref, jr_ref, z_ref, jc_ref, lr_ref,
    a_hi, a_lo, jt_hi, jt_lo, jc_hi, jc_lo, lr_hi, lr_lo, l_tile, o_tile,
    own_v, a_stage, j_stage, c_stage, l_stage,
    stage_sem, own_sem,
    ap_send, ap_recv, jr_send, jr_recv,
    zu_send, zu_recv, zd_send, zd_recv,
    ju_send, jd_send, jc_recv, jp_send, jp_recv,
    lr_send, lr_recv, o_send, o_recv,
):
    rows_n, cols_n, pair_dev, width, block, half, piece = size
    order = 2 * block
    tiles = half // LANES
    per_row = width * tiles
    r = lax.axis_index("row")
    c = lax.axis_index("col")
    l = lax.axis_index("layer")
    other = 1 - l
    partner = (r, c, other)
    pending = []

    def remote(src, dst, send, recv, device):
        return pltpu.make_async_remote_copy(
            src_ref=src, dst_ref=dst, send_sem=send, recv_sem=recv, device_id=device, device_id_type=MESH
        )

    def send(copy, condition=None):
        if condition is None:
            copy.start()
        else:
            pl.when(condition)(copy.start)
        pending.append((copy, condition))

    def lanes(start, count):
        return pl.ds(pl.multiple_of(start, LANES), count)

    barrier = pltpu.get_barrier_semaphore()
    for mask in range(cols_n):
        for layer in (l, other):
            if mask == 0 and layer is l:
                continue
            pl.semaphore_signal(barrier, inc=1, device_id=(r, c ^ mask, layer), device_id_type=MESH)
    has_next = r + 1 < rows_n
    has_prev = r > 0

    @pl.when(has_next)
    def _():
        pl.semaphore_signal(barrier, inc=1, device_id=(r + 1, c, l), device_id_type=MESH)

    @pl.when(has_prev)
    def _():
        pl.semaphore_signal(barrier, inc=1, device_id=(r - 1, c, l), device_id_type=MESH)

    pl.semaphore_wait(barrier, 2 * cols_n - 1 + has_next.astype(jnp.int32) + has_prev.astype(jnp.int32))

    for p in range(pair_dev):
        send(remote(t_ref.at[p], z_ref.at[r, p], zu_send.at[0, p], zu_recv.at[1, p], (r + 1, c, l)), has_next)
        send(remote(t_ref.at[p], z_ref.at[r, p], zd_send.at[0, p], zd_recv.at[1, p], (r - 1, c, l)), has_prev)

    def part(m, layer):
        return lanes(m * block + layer * half, half)

    mine = c * 2 + l
    for mask in list(range(1, cols_n)) + [0]:
        for s, layer in ((0, l), (1, other)):
            if mask == 0 and s == 0:
                continue
            for m in range(2):
                send(remote(
                    t_ref.at[:, :, part(m, layer)],
                    jr_ref.at[:, m, pl.ds(mine * piece, piece), :],
                    jr_send.at[mask, s, m], jr_recv.at[mask, s, m], (r, c ^ mask, layer),
                ))

    raw = pair_dev * order * per_row // pair_dev
    for p in range(pair_dev):
        rows = pl.ds(p * raw, raw)
        send(remote(a_ref.at[rows, :], ap_ref.at[rows, :], ap_send.at[p], ap_recv.at[p], partner))

    for p in range(pair_dev):
        send(remote(
            t_ref.at[p], jc_ref.at[mine, p], ju_send.at[0, p], jc_recv.at[c ^ r, p], (r, r, l)
        ), c != r)

    load = pltpu.make_async_copy(t_ref, own_v, own_sem.at[0])
    load.start()
    load.wait()
    fills = [pltpu.make_async_copy(own_v, z_ref.at[r], own_sem.at[0])]
    for m in range(2):
        fills.append(pltpu.make_async_copy(
            own_v.at[:, :, part(m, l)], jr_ref.at[:, m, pl.ds(mine * piece, piece), :], own_sem.at[1 + m]
        ))
    for copy in fills:
        copy.start()

    def split_columns(src, layer, first):
        chunk = ROWS * per_row
        count = order // ROWS

        def fetch(at):
            slot = lax.rem(at, 2)
            rows = pl.ds(pl.multiple_of((first + at) * chunk, chunk), chunk)
            return pltpu.make_async_copy(src.at[rows, :], a_stage.at[slot], stage_sem.at[slot])

        fetch(0).start()

        def body(at, carry):
            @pl.when(at + 1 < count)
            def _():
                fetch(at + 1).start()

            fetch(at).wait()
            slot = lax.rem(at, 2)
            rows = pl.ds(pl.multiple_of(at * ROWS, ROWS), ROWS)
            for j in range(width):
                for tile in range(tiles):
                    x = a_stage[slot, pl.ds(tile * width + j, ROWS, per_row), :]
                    high, low = halves_of(x)
                    cols = lanes(j * block + layer * half + tile * LANES, LANES)
                    a_hi[first // count, rows, cols] = high
                    a_lo[first // count, rows, cols] = low
            return carry

        lax.fori_loop(0, count, body, 0)

    for p in range(pair_dev):
        split_columns(a_ref, l, p * (order // ROWS))
    for copy in fills:
        copy.wait()
    for p in range(pair_dev):
        rows = pl.ds(p * raw, raw)
        remote(a_ref.at[rows, :], ap_ref.at[rows, :], ap_send.at[p], ap_recv.at[p], partner).wait_recv()
        split_columns(ap_ref, other, p * (order // ROWS))

    def forward(step):
        for p in range(pair_dev):
            for recv, snd, plane, to, into in (
                (zu_recv, zu_send, r - step, r + 1, ju_send),
                (zd_recv, zd_send, r + step, r - 1, jd_send),
            ):
                here = (plane >= 0) & (plane < rows_n)
                onward = here & (to >= 0) & (to < rows_n)
                at = jnp.clip(plane, 0, rows_n - 1)
                block_ref = z_ref.at[at, p]

                @pl.when(here)
                def _():
                    remote(block_ref, block_ref, snd.at[step, p], recv.at[step, p], partner).wait_recv()

                if step + 1 < rows_n:
                    send(remote(block_ref, block_ref, snd.at[step, p], recv.at[step + 1, p], (to, c, l)), onward)
                send(remote(
                    block_ref, jc_ref.at[mine, p], into.at[step, p], jc_recv.at[c ^ at, p], (r, at, l)
                ), here & (at != c))

    early = max(rows_n - 2, 1)
    forward(1)

    wide = 2 * piece
    for mask in range(cols_n):
        for s, layer in ((0, l), (1, other)):
            if mask == 0 and s == 0:
                continue
            for m in range(2):
                sender = (c ^ mask) * 2 + layer
                remote(
                    t_ref.at[:, :, part(m, layer)],
                    jr_ref.at[:, m, pl.ds(sender * piece, piece), :],
                    jr_send.at[mask, s, m], jr_recv.at[mask, s, m], partner,
                ).wait_recv()
        at = lanes((c ^ mask) * wide, wide)
        fetch = pltpu.make_async_copy(jr_ref.at[:, :, at, :], j_stage, stage_sem.at[0])
        fetch.start()
        fetch.wait()

        def turn(index, carry):
            p, m = lax.div(index, 2), lax.rem(index, 2)
            high, low = halves_of(j_stage[p, m].T)
            jt_hi[index, :, at] = high
            jt_lo[index, :, at] = low
            return carry

        lax.fori_loop(0, width, turn, 0)

    for step in range(2, early + 1):
        forward(step)

    def left(slot):
        p = slot // 2
        if slot == 1:
            moved, target, at = has_prev, r - 1, jnp.where(has_prev, 3, 2)
        elif slot == width - 2:
            moved, target, at = has_next, r + 1, jnp.where(has_next, 0, 3)
        else:
            moved, target, at = None, r, (jnp.where(has_prev, 2, 0) if slot == 0 else 1)

        def copies(n):
            src, dst = l_tile.at[slot * width + n], lr_ref.at[at, n]
            there = remote(src, dst, lr_send.at[slot, n], lr_recv.at[at, n], (target, c, l))
            here = pltpu.make_async_copy(src, dst, lr_recv.at[at, n])
            return there, here

        def body(n, carry):
            cols = lanes(n * block, block)
            l_tile[slot * width + n] = three_dots(
                jt_hi[slot], jt_lo[slot], a_hi[p, :, cols], a_lo[p, :, cols]
            )
            there, here = copies(n)
            if moved is None:
                here.start()
            else:
                pl.when(moved)(there.start)
                pl.when(jnp.logical_not(moved))(here.start)
            return carry

        lax.fori_loop(0, width, body, 0)
        if moved is not None:
            for n in range(width):
                pending.append((copies(n)[0], moved))

    left(width - 2)
    left(1)
    left(0)
    left(width - 1)
    for step in range(early + 1, rows_n):
        forward(step)

    def right_pieces(p):
        todo = []
        for mask in list(range(1, cols_n)) + [0]:
            index = (c ^ mask) * 2 + l
            src = jc_ref.at[index, p] if mask else z_ref.at[c, p]
            if mask:
                remote(src, src, jp_send.at[mask, p], jc_recv.at[mask, p], partner).wait_recv()
            copy = remote(src, jc_ref.at[index, p], jp_send.at[mask, p], jp_recv.at[mask, p], partner)
            send(copy)
            todo.append((src, index, None))
        for mask in list(range(1, cols_n)) + [0]:
            index = (c ^ mask) * 2 + other
            src = jc_ref.at[index, p]
            todo.append((src, index, remote(src, src, jp_send.at[mask, p], jp_recv.at[mask, p], partner)))

        def fetch(n):
            src, _, copy = todo[n]
            if copy is not None:
                copy.wait_recv()
            load = pltpu.make_async_copy(src, c_stage.at[n % 2], stage_sem.at[n % 2])
            load.start()
            return load

        loads = [fetch(0)]
        for n, (_, index, _) in enumerate(todo):
            if n + 1 < len(todo):
                loads.append(fetch(n + 1))
            loads[n].wait()
            high, low = halves_of(c_stage[n % 2])
            rows = pl.ds(pl.multiple_of(index * piece, piece), piece)
            jc_hi[p, rows, :] = high
            jc_lo[p, rows, :] = low

    def left_rows(at):
        def fetch(n):
            slot = lax.rem(n, 2)
            return pltpu.make_async_copy(lr_ref.at[at, n], l_stage.at[slot], stage_sem.at[slot])

        def arrived(n):
            pltpu.make_async_copy(lr_ref.at[at, n], lr_ref.at[at, n], lr_recv.at[at, n]).wait()

        arrived(0)
        fetch(0).start()

        def body(n, carry):
            @pl.when(n + 1 < width)
            def _():
                arrived(n + 1)
                fetch(n + 1).start()

            fetch(n).wait()
            high, low = halves_of(l_stage[lax.rem(n, 2)])
            cols = lanes(n * block, block)
            lr_hi[at, :, cols] = high
            lr_lo[at, :, cols] = low
            return carry

        lax.fori_loop(0, width, body, 0)

    left_end, right_end = c > 0, c + 1 < cols_n

    def right(at, j):
        q, m = j // 2, j % 2
        rows = slice(q * order, (q + 1) * order)
        cols = slice(m * block, (m + 1) * block)
        tile = at * width + j
        o_tile[tile] = three_dots(
            lr_hi[at, :, rows], lr_lo[at, :, rows], jc_hi[q, :, cols], jc_lo[q, :, cols]
        )
        if j == 1:
            moved, target, slot = left_end, c - 1, jnp.where(left_end, 3, 2)
        elif j == width - 2:
            moved, target, slot = right_end, c + 1, jnp.where(right_end, 0, 3)
        else:
            moved, target, slot = None, c, (jnp.where(left_end, 2, 0) if j == 0 else 1)
        dst = out_ref.at[slot, at, pl.ds(pl.multiple_of(l * half, half), half), :]
        column = c if moved is None else jnp.where(moved, target, c)
        for s, layer in ((0, l), (1, other)):
            src = o_tile.at[tile, :, lanes(layer * half, half)]
            there = remote(src, dst, o_send.at[tile, s], o_recv.at[slot, l], (r, column, layer))
            if s == 1:
                send(there)
                continue
            here = pltpu.make_async_copy(src, dst, o_recv.at[slot, l])
            if moved is None:
                here.start()
            else:
                send(there, moved)
                pl.when(jnp.logical_not(moved))(here.start)

    staying, arriving = (1, width - 2), (0, width - 1)
    for at in staying:
        left_rows(at)
    for q in range(pair_dev):
        right_pieces(q)
        for at in staying:
            for j in ((1, 0) if q == 0 else (2, 3)):
                right(at, j)
    for at in arriving:
        left_rows(at)
        for j in (1, 2, 0, 3):
            right(at, j)

    for slot in range(width):
        for layer in range(2):
            block_ref = out_ref.at[slot, :, pl.ds(layer * half, half), :]
            pltpu.make_async_copy(block_ref, block_ref, o_recv.at[slot, layer]).wait()
    for copy, condition in pending:
        if condition is None:
            copy.wait_send()
        else:
            pl.when(condition)(copy.wait_send)


def spread(width, tiles, x_ref, o_ref):
    rows = x_ref.shape[2]
    for j in range(width):
        for tile in range(tiles):
            o_ref[pl.ds(tile * width + j, rows, width * tiles), :] = x_ref[j, 0, :, tile * LANES : (tile + 1) * LANES]


def shards(matrix, transforms):
    width, block, _, half = matrix.shape
    pair_dev = width // 2
    order = 2 * block
    rows_n, cols_n = lax.axis_size("row"), lax.axis_size("col")
    tiles = half // LANES
    per_row = width * tiles
    raw_rows = width * block * per_row
    own = transforms[0]
    piece = own.shape[1]
    pieces = 2 * cols_n
    f32, bf16 = jnp.float32, jnp.bfloat16

    raw = matrix.reshape(width * block, width, tiles, LANES).transpose(0, 2, 1, 3).reshape(raw_rows, LANES)
    any_space = pl.BlockSpec(memory_space=pl.ANY)
    dma = pltpu.SemaphoreType.DMA
    flops = 3 * 2 * 2 * width * half * order * width * block
    outs = pl.pallas_call(
        functools.partial(sweep, (rows_n, cols_n, pair_dev, width, block, half, piece)),
        name="sweep",
        out_shape=[
            jax.ShapeDtypeStruct((width, width, block, half), f32),
            jax.ShapeDtypeStruct((raw_rows, LANES), f32),
            jax.ShapeDtypeStruct((pair_dev, 2, order, half), f32),
            jax.ShapeDtypeStruct((rows_n, pair_dev, piece, order), f32),
            jax.ShapeDtypeStruct((pieces, pair_dev, piece, order), f32),
            jax.ShapeDtypeStruct((width, width, half, block), f32),
        ],
        in_specs=[any_space, any_space],
        out_specs=[any_space] * 6,
        scratch_shapes=[
            pltpu.VMEM((pair_dev, order, width * block), bf16),
            pltpu.VMEM((pair_dev, order, width * block), bf16),
            pltpu.VMEM((width, half, order), bf16),
            pltpu.VMEM((width, half, order), bf16),
            pltpu.VMEM((pair_dev, order, order), bf16),
            pltpu.VMEM((pair_dev, order, order), bf16),
            pltpu.VMEM((width, half, width * block), bf16),
            pltpu.VMEM((width, half, width * block), bf16),
            pltpu.VMEM((width * width, half, block), f32),
            pltpu.VMEM((width * width, half, block), f32),
            pltpu.VMEM((pair_dev, piece, order), f32),
            pltpu.VMEM((2, ROWS * per_row, LANES), f32),
            pltpu.VMEM((pair_dev, 2, 2 * piece, half), f32),
            pltpu.VMEM((2, piece, order), f32),
            pltpu.VMEM((2, half, block), f32),
            dma((2,)), dma((3,)),
            dma((pair_dev,)), dma((pair_dev,)),
            dma((cols_n, 2, 2)), dma((cols_n, 2, 2)),
            dma((rows_n, pair_dev)), dma((rows_n, pair_dev)), dma((rows_n, pair_dev)), dma((rows_n, pair_dev)),
            dma((rows_n, pair_dev)), dma((rows_n, pair_dev)), dma((cols_n, pair_dev)),
            dma((cols_n, pair_dev)), dma((cols_n, pair_dev)),
            dma((width, width)), dma((width, width)),
            dma((width * width, 2)), dma((width, 2)),
        ],
        compiler_params=pltpu.CompilerParams(
            collective_id=0, has_side_effects=True, vmem_limit_bytes=VMEM_LIMIT
        ),
        cost_estimate=pl.CostEstimate(flops=flops, bytes_accessed=0, transcendentals=0),
    )(raw, own)
    blocks = outs[0]

    rows = 256
    steps = block // rows
    result = pl.pallas_call(
        functools.partial(spread, width, tiles),
        name="spread",
        grid=(width, steps),
        in_specs=[pl.BlockSpec((width, 1, rows, half), lambda i, a: (0, i, a, 0))],
        out_specs=pl.BlockSpec((rows * per_row, LANES), lambda i, a: (i * steps + a, 0)),
        out_shape=jax.ShapeDtypeStruct((raw_rows, LANES), f32),
    )(blocks)
    result = result.reshape(width, block, tiles, width, LANES).transpose(0, 1, 3, 2, 4)
    return result.reshape(width, block, width, half)


def solution(mesh):
    return jax.shard_map(
        shards,
        mesh=mesh,
        in_specs=(P("row", None, "col", "layer"), P(None, "row", ("col", "layer"), None)),
        out_specs=P("row", None, "col", "layer"),
        check_vma=False,
    )
```

profile of v0, /device:TPU:5, one launch (start us, length us, event | category | flops | bytes accessed | tf_op | source)
XLA Modules:
  0.0 213.1 jit_solution(1993494685873239763)
XLA Ops:
  0.0 203.4 %sweep.1 = (f32[4,4,512,256]{3,2,1,0:T(8,128)}, f32[16384,128]{1,0:T(8,128)}, f32[2,2,1024,256]{3,2,1,0:T(8,128)}, f32[4,2,128,1024]{3,2,1,0:T(8,128)}, f32[8,2,...) custom-call(f32[16384,128]{1,0:T(8,128)} %bitcast.11, f32[2,128,1024]{2,1,0:T(8,128)} %bitcast.12), custom_call_target="tpu_custom_call" | custom-call | flops 25769803776 | tf_op jit(solution)/shard_map/sweep/pallas_call | solution.py:396
  203.4 9.7 %spread.1 = f32[16384,128]{1,0:T(8,128)} custom-call(f32[4,4,512,256]{3,2,1,0:T(8,128)} %get-tuple-element.6.x_ref), custom_call_target="tpu_custom_call" | custom-call | tf_op jit(solution)/shard_map/spread/pallas_call | solution.py:443
where the time goes:
time: 214 us; the launch traced here: 213 us
  Pallas kernels  213 us (100%)
    pallas_call x1, Pallas kernels, shards(): pl.pallas_call(functools.partial(sweep, (rows_n, cols_n, pair_dev, width,...  203 us
    pallas_call x1, Pallas kernels, shards(): pl.pallas_call(functools.partial(spread, width, tiles), name='spread', gr...  9.7 us

commit v1 on v0

v1 whole, which is shorter than its diff:
```python
import functools

import jax
import jax.numpy as jnp
from jax import lax
from jax.experimental import pallas as pl
from jax.experimental.pallas import tpu as pltpu
from jax.sharding import PartitionSpec as P

MESH = pl.DeviceIdType.MESH
LANES = 128
ROWS = 256
VMEM_LIMIT = 66_000_000
scope = jax.named_scope


def halves_of(x):
    high = x.astype(jnp.bfloat16)
    low = (x - high.astype(jnp.float32)).astype(jnp.bfloat16)
    return high, low


def three_dots(a_high, a_low, b_high, b_low):
    def dot(a, b):
        return lax.dot_general(a, b, (((1,), (0,)), ((), ())), preferred_element_type=jnp.float32)

    return dot(a_high, b_high) + (dot(a_high, b_low) + dot(a_low, b_high))


def sweep(
    size,
    a_ref, t_ref,
    out_ref, ap_ref, jr_ref, jo_ref, z_ref, jc_ref, lr_ref, via_ref,
    a_hi, a_lo, jt_hi, jt_lo, jc_hi, jc_lo, lr_hi, lr_lo, l_tile, o_tile,
    own_v, a_stage, j_stage, c_stage, l_stage,
    stage_sem, c_sem, own_sem,
    ap_send, ap_recv, jr_send, jr_recv,
    zu_send, zu_recv, zd_send, zd_recv,
    ju_send, jd_send, jc_recv, jp_send, jp_recv, jo_send, jo_recv,
    lr_send, lr_recv, o_send, o_recv, via_send, via_recv,
):
    rows_n, cols_n, pair_dev, width, block, half, piece = size
    order = 2 * block
    tiles = half // LANES
    r = lax.axis_index("row")
    c = lax.axis_index("col")
    l = lax.axis_index("layer")
    other = 1 - l
    partner = (r, c, other)
    mine = c * 2 + l
    square = cols_n == 4
    pending = []

    def remote(src, dst, send, recv, device):
        return pltpu.make_async_remote_copy(
            src_ref=src, dst_ref=dst, send_sem=send, recv_sem=recv, device_id=device, device_id_type=MESH
        )

    def send(copy, condition=None):
        if condition is None:
            copy.start()
        else:
            pl.when(condition)(copy.start)
        pending.append((copy, condition))

    def lanes(start, count):
        return pl.ds(pl.multiple_of(start, LANES), count)

    def member(s, p):
        return 1 - p if s == 0 else p

    def slot_of(s, p):
        return 2 * p + member(s, p)

    barrier = pltpu.get_barrier_semaphore()
    for mask in range(cols_n):
        for layer in (l, other):
            if mask == 0 and layer is l:
                continue
            pl.semaphore_signal(barrier, inc=1, device_id=(r, c ^ mask, layer), device_id_type=MESH)
    has_next = r + 1 < rows_n
    has_prev = r > 0

    @pl.when(has_next)
    def _():
        pl.semaphore_signal(barrier, inc=1, device_id=(r + 1, c, l), device_id_type=MESH)

    @pl.when(has_prev)
    def _():
        pl.semaphore_signal(barrier, inc=1, device_id=(r - 1, c, l), device_id_type=MESH)

    with scope("barrier"):
        pl.semaphore_wait(barrier, 2 * cols_n - 1 + has_next.astype(jnp.int32) + has_prev.astype(jnp.int32))

    def own_half(s, p):
        return t_ref.at[p, :, pl.ds(member(s, p) * block, block)]

    def rows_out(s):
        for p in range(pair_dev):
            send(remote(
                own_half(s, p), z_ref.at[r, s, p], zu_send.at[0, s, p], zu_recv.at[1, s, p], (r + 1, c, l)
            ), has_next)
            send(remote(
                own_half(s, p), z_ref.at[r, s, p], zd_send.at[0, s, p], zd_recv.at[1, s, p], (r - 1, c, l)
            ), has_prev)

    def part(m, layer):
        return lanes(m * block + layer * half, half)

    def plane_copy(mask, side, s, p, origin, source, device):
        m = member(s, p)
        dst = jr_ref.at[p, m, pl.ds(pl.multiple_of(origin * piece, piece), piece), :]
        return remote(source if source is not None else dst, dst, jr_send.at[mask, side, s, p],
                      jr_recv.at[mask, side, s, p], device)

    def plane_out(s, masks, pairs=range(pair_dev)):
        for mask in masks:
            for p in pairs:
                for side, layer in ((0, l), (1, other)):
                    if mask == 0 and side == 0:
                        continue
                    src = t_ref.at[p, :, part(member(s, p), layer)]
                    send(plane_copy(mask, side, s, p, mine, src, (r, c ^ mask, layer)))

    seen = set()

    def plane_wait(mask, s, p):
        if (mask, s, p) in seen:
            return
        seen.add((mask, s, p))
        for side, layer in ((0, l), (1, other)):
            if mask == 0 and side == 0:
                continue
            plane_copy(mask, side, s, p, (c ^ mask) * 2 + layer, None, partner).wait_recv()

    def plane_relay(s, p, mask):
        plane_wait(mask, s, p)
        for side, layer in ((0, l), (1, other)):
            send(plane_copy(3, side, s, p, (c ^ mask) * 2 + layer, None, (r, c ^ mask ^ 3, l)))

    same = r == c
    differs = r != c

    def other_half(s, p):
        src = jr_ref.at[p, member(s, p)]
        return remote(src, jo_ref.at[p, member(s, p)], jo_send.at[s, p], jo_recv.at[s, p], partner)

    def halves_out(s):
        for p in range(pair_dev):
            send(other_half(s, p), same)

    def arrivals(step):
        for recv, snd, plane, to, into in (
            (zu_recv, zu_send, r - step, r + 1, ju_send),
            (zd_recv, zd_send, r + step, r - 1, jd_send),
        ):
            here = (plane >= 0) & (plane < rows_n)
            onward = here & (to >= 0) & (to < rows_n)
            yield recv, snd, jnp.clip(plane, 0, rows_n - 1), here, onward, to, into

    def hand_over(s, step, among, neighbours=(True, False)):
        for near in neighbours:
            for p in range(pair_dev):
                for _, _, at, here, onward, _, into in arrivals(step):
                    chosen = (onward if among else here & jnp.logical_not(onward)) & (at != c)
                    chosen = chosen & ((at == (c ^ 1)) if near else (at != (c ^ 1)))
                    send(remote(
                        z_ref.at[at, s, p], jc_ref.at[mine, s, p], into.at[step, s, p], jc_recv.at[c ^ at, s, p],
                        (r, at, l),
                    ), chosen)

    def forward(s, step):
        for p in range(pair_dev):
            for recv, snd, at, _, onward, to, _ in arrivals(step):
                block_ref = z_ref.at[at, s, p]
                if step + 1 == rows_n:
                    continue

                @pl.when(onward)
                def _():
                    remote(block_ref, block_ref, snd.at[step, s, p], recv.at[step, s, p], partner).wait_recv()

                send(remote(
                    block_ref, block_ref, snd.at[step, s, p], recv.at[step + 1, s, p], (to, c, l)
                ), onward)

    def finish(s, step):
        for p in range(pair_dev):
            for recv, snd, at, here, onward, _, _ in arrivals(step):
                block_ref = z_ref.at[at, s, p]

                @pl.when(here & jnp.logical_not(onward))
                def _():
                    remote(block_ref, block_ref, snd.at[step, s, p], recv.at[step, s, p], partner).wait_recv()

        hand_over(s, step, False)

    def columns_copy(p):
        rows = pl.ds(p * order, order)
        return remote(a_ref.at[rows], ap_ref.at[rows], ap_send.at[p], ap_recv.at[p], partner)

    def split_columns(src, layer, p):
        count = order // ROWS

        def fetch(at):
            slot = lax.rem(at, 2)
            rows = pl.ds(pl.multiple_of(p * order + at * ROWS, ROWS), ROWS)
            for j in range(width):
                for tile in range(tiles):
                    pltpu.make_async_copy(
                        src.at[rows, tile * width + j, 0, :],
                        a_stage.at[slot, :, pl.ds(j * half + tile * LANES, LANES)],
                        stage_sem.at[slot],
                    ).start()

        def body(at, carry):
            @pl.when(at + 1 < count)
            def _():
                fetch(at + 1)

            slot = lax.rem(at, 2)
            pltpu.make_async_copy(a_stage.at[slot], a_stage.at[slot], stage_sem.at[slot]).wait()
            rows = pl.ds(pl.multiple_of(at * ROWS, ROWS), ROWS)
            for j in range(width):
                high, low = halves_of(a_stage[slot, :, j * half : (j + 1) * half])
                cols = lanes(j * block + layer * half, half)
                a_hi[p, rows, cols] = high
                a_lo[p, rows, cols] = low
            return carry

        fetch(0)
        lax.fori_loop(0, count, body, 0)

    wide = 2 * piece

    def turn(s):
        def fetch(mask):
            for p in range(pair_dev):
                plane_wait(mask, s, p)
            at = pl.ds(pl.multiple_of((c ^ mask) * wide, wide), wide)
            for p in range(pair_dev):
                pltpu.make_async_copy(
                    jr_ref.at[p, member(s, p), at, :], j_stage.at[mask % 2, p], stage_sem.at[mask % 2]
                ).start()

        fetch(0)
        for mask in range(cols_n):
            if mask + 1 < cols_n:
                fetch(mask + 1)
            stage = j_stage.at[mask % 2]
            pltpu.make_async_copy(stage, stage, stage_sem.at[mask % 2]).wait()
            at = lanes((c ^ mask) * wide, wide)
            for p in range(pair_dev):
                high, low = halves_of(j_stage[mask % 2, p].T)
                jt_hi[slot_of(s, p), :, at] = high
                jt_lo[slot_of(s, p), :, at] = low

    def left(slot):
        p = slot // 2

        def body(n, carry):
            cols = lanes(n * block, block)
            l_tile[slot * width + n] = three_dots(
                jt_hi[slot], jt_lo[slot], a_hi[p, :, cols], a_lo[p, :, cols]
            )
            return carry

        lax.fori_loop(0, width, body, 0)

    def left_out(slot, order_of_tiles):
        if slot == 1:
            moved, target, at = has_prev, r - 1, jnp.where(has_prev, 3, 2)
        elif slot == width - 2:
            moved, target, at = has_next, r + 1, jnp.where(has_next, 0, 3)
        else:
            moved, target, at = None, r, (jnp.where(has_prev, 2, 0) if slot == 0 else 1)
        for n in order_of_tiles:
            src, dst = l_tile.at[slot * width + n], lr_ref.at[at, n]
            here = pltpu.make_async_copy(src, dst, lr_recv.at[at, n])
            if moved is None:
                here.start()
            else:
                send(remote(src, dst, lr_send.at[slot, n], lr_recv.at[at, n], (target, c, l)), moved)
                pl.when(jnp.logical_not(moved))(here.start)

    def right_pieces(s):
        masks = list(range(1, cols_n)) + [0]
        deep = c_stage.shape[0]

        def handed(mask, index, src):
            return remote(src, jc_ref.at[index, s], jp_send.at[mask, s], jp_recv.at[mask, s], partner)

        todo = []
        for mask in masks:
            index = (c ^ mask) * 2 + l
            src = jc_ref.at[index, s] if mask else z_ref.at[c, s]
            copy = handed(mask, index, src)
            todo.append((src, index, mask, copy, True))
            pending.append((copy, differs))
        for mask in masks:
            index = (c ^ mask) * 2 + other
            src = jc_ref.at[index, s]
            todo.append((src, index, mask, handed(mask, index, src), False))

        def fetch(n):
            src, _, _, copy, first_hand = todo[n]
            if not first_hand:
                copy.wait_recv()
            load = pltpu.make_async_copy(src, c_stage.at[n % deep], c_sem.at[n % deep])
            load.start()
            return load

        @pl.when(differs)
        def _():
            for src, index, mask, copy, first_hand in todo:
                if first_hand:
                    if mask:
                        for p in range(pair_dev):
                            got = jc_ref.at[index, s, p]
                            remote(got, got, jp_send.at[mask, s], jc_recv.at[mask, s, p], partner).wait_recv()
                    copy.start()
            loads = [fetch(n) for n in range(deep - 1)]
            for n, (_, index, _, _, _) in enumerate(todo):
                if n + deep - 1 < len(todo):
                    loads.append(fetch(n + deep - 1))
                loads[n].wait()
                rows = pl.ds(pl.multiple_of(index * piece, piece), piece)
                for p in range(pair_dev):
                    high, low = halves_of(c_stage[n % deep, p])
                    jc_hi[slot_of(s, p), rows, :] = high
                    jc_lo[slot_of(s, p), rows, :] = low

        @pl.when(same)
        def _():
            jobs = [(side, n) for side in range(2) for n in range(cols_n)]

            def fetch(k):
                side, n = jobs[k]
                if side == 1 and n == 0:
                    for p in range(pair_dev):
                        other_half(s, p).wait_recv()
                for p in range(pair_dev):
                    src = (jo_ref if side else jr_ref).at[p, member(s, p), pl.ds(n * wide, wide), :]
                    pltpu.make_async_copy(src, j_stage.at[k % 2, p], stage_sem.at[k % 2]).start()

            fetch(0)
            for k, (side, n) in enumerate(jobs):
                if k + 1 < len(jobs):
                    fetch(k + 1)
                stage = j_stage.at[k % 2]
                pltpu.make_async_copy(stage, stage, stage_sem.at[k % 2]).wait()
                cols = lanes((other if side else l) * half, half)
                for p in range(pair_dev):
                    high, low = halves_of(j_stage[k % 2, p])
                    jc_hi[slot_of(s, p), n * wide : (n + 1) * wide, cols] = high
                    jc_lo[slot_of(s, p), n * wide : (n + 1) * wide, cols] = low

    def left_rows(at, q):
        loads = []
        for n in (2 * q, 2 * q + 1):
            src = lr_ref.at[at, n]
            pltpu.make_async_copy(src, src, lr_recv.at[at, n]).wait()
            loads.append(pltpu.make_async_copy(src, l_stage.at[n % 2], stage_sem.at[n % 2]))
            loads[-1].start()
        for n in (2 * q, 2 * q + 1):
            loads[n % 2].wait()
            high, low = halves_of(l_stage[n % 2])
            cols = slice(n * block, (n + 1) * block)
            lr_hi[at, :, cols] = high
            lr_lo[at, :, cols] = low

    left_end, right_end = c > 0, c + 1 < cols_n
    staying, arriving = (1, width - 2), (0, width - 1)
    by_way = (staying[0], arriving[0]) if square else ()
    low_rows = pl.ds(pl.multiple_of(l * half, half), half)

    def right(at, j):
        q = j // 2
        rows = slice(q * order, (q + 1) * order)
        tile = at * width + j
        o_tile[tile] = three_dots(lr_hi[at, :, rows], lr_lo[at, :, rows], jc_hi[j], jc_lo[j])
        around = None
        if j == 1:
            moved, target, slot = left_end, c - 1, jnp.where(left_end, 3, 2)
            if at in by_way:
                around = c == 2
        elif j == width - 2:
            moved, target, slot = right_end, c + 1, jnp.where(right_end, 0, 3)
            if at in by_way:
                around = c == 1
        else:
            moved, target, slot = None, c, (jnp.where(left_end, 2, 0) if j == 0 else 1)
        dst = out_ref.at[slot, at, low_rows, :]
        column = c if moved is None else jnp.where(moved, target, c)
        for s, layer in ((0, l), (1, other)):
            src = o_tile.at[tile, :, lanes(layer * half, half)]
            condition = moved if s == 0 else None
            if around is not None:
                index = by_way.index(at)
                send(remote(
                    src, via_ref.at[index, l], o_send.at[tile, s], via_recv.at[index, l], (r, c ^ 2, layer)
                ), around)
                direct = jnp.logical_not(around)
                condition = direct if condition is None else condition & direct
            if s == 1 or moved is not None:
                send(remote(src, dst, o_send.at[tile, s], o_recv.at[slot, l], (r, column, layer)), condition)
            if s == 0:
                here = pltpu.make_async_copy(src, dst, o_recv.at[slot, l])
                if moved is None:
                    here.start()
                else:
                    pl.when(jnp.logical_not(moved))(here.start)

    def right_relay(index):
        outer = (c == 0) | (c == cols_n - 1)
        slot = jnp.where(c == 0, 3, 0)
        for layer in range(2):
            src = via_ref.at[index, layer]
            rows = pl.ds(layer * half, half)

            @pl.when(outer)
            def _():
                remote(src, src, via_send.at[index, layer], via_recv.at[index, layer], partner).wait_recv()

            send(remote(
                src, out_ref.at[slot, by_way[index], rows, :], via_send.at[index, layer], o_recv.at[slot, layer],
                (r, c ^ 1, l),
            ), outer)

    rows_out(0)
    if square:
        plane_out(0, (1, 2, 0))
        plane_out(1, (1, 0))
    else:
        for s in range(2):
            plane_out(s, list(range(1, cols_n)) + [0])
    for p in range(pair_dev):
        send(columns_copy(p))
    load = pltpu.make_async_copy(t_ref, own_v, own_sem.at[0, 0, 0])
    load.start()
    load.wait()
    fills = []
    for s in range(2):
        for p in range(pair_dev):
            m = member(s, p)
            fills.append(pltpu.make_async_copy(
                own_v.at[p, :, pl.ds(m * block, block)], z_ref.at[r, s, p], own_sem.at[0, s, p]
            ))
            fills.append(pltpu.make_async_copy(
                own_v.at[p, :, part(m, l)],
                jr_ref.at[p, m, pl.ds(pl.multiple_of(mine * piece, piece), piece), :], own_sem.at[1, s, p]
            ))
    for copy in fills:
        copy.start()
    with scope("split_own"):
        for p in range(pair_dev):
            split_columns(a_ref, l, p)
    for copy in fills:
        copy.wait()
    if square:
        with scope("relay0"):
            for p in range(pair_dev):
                plane_relay(0, p, 1)
        plane_out(1, (2,), (1, 0))
    with scope("fwd_a1"):
        forward(0, 1)
        hand_over(0, 1, True, (True,))
    with scope("split_p0"):
        columns_copy(0).wait_recv()
        split_columns(ap_ref, other, 0)
    with scope("split_p1"):
        for p in range(1, pair_dev):
            columns_copy(p).wait_recv()
            split_columns(ap_ref, other, p)
    for step in range(2, rows_n - 1):
        with scope("fwd_a2"):
            forward(0, step)
            hand_over(0, step, True, (True,))
    rows_out(1)
    if square:
        with scope("relay1"):
            plane_relay(1, 0, 1)
    for step in range(1, rows_n - 1):
        hand_over(0, step, True, (False,))
    with scope("turn_a"):
        turn(0)
    halves_out(0)
    with scope("left_a2"):
        left(width - 2)
    for step in range(1, rows_n):
        with scope("fin_a"):
            finish(0, step)
    if square:
        with scope("relay2"):
            plane_relay(1, 1, 2)
    with scope("fwd_b1"):
        forward(1, 1)
        hand_over(1, 1, True)
    with scope("left_a1"):
        left(1)
    with scope("turn_b"):
        turn(1)
    halves_out(1)
    for step in range(2, rows_n - 1):
        with scope("fwd_b2"):
            forward(1, step)
            hand_over(1, step, True)
    first, last = (0, 1), (2, 3)
    for tiles_first, tiles_last in ((first, last), (last, first)):
        left_out(width - 2, tiles_first)
        left_out(1, tiles_last)
    with scope("left_b"):
        for slot in (0, width - 1):
            left(slot)
            left_out(slot, range(width))
    for at in staying:
        with scope("rows"):
            for q in range(pair_dev):
                left_rows(at, q)
    for step in range(1, rows_n):
        with scope("fin_b"):
            finish(1, step)
    with scope("pieces_a"):
        right_pieces(0)
    moving = (1, width - 2)
    for at in staying:
        with scope("right"):
            for j in moving:
                right(at, j)
    for at, q in ((0, 0), (width - 1, 1)):
        with scope("rows_arr"):
            left_rows(at, q)
        with scope("right"):
            right(at, moving[q])
    with scope("pieces_b"):
        right_pieces(1)
    if square:
        with scope("via0"):
            right_relay(0)
    for at, q in ((0, 1), (width - 1, 0)):
        with scope("rows_arr"):
            left_rows(at, q)
        with scope("right"):
            right(at, moving[q])
    with scope("right_local"):
        for at in staying:
            for j in (0, width - 1):
                right(at, j)
    if square:
        with scope("via1"):
            right_relay(1)
    with scope("right_local"):
        for at in arriving:
            for j in (0, width - 1):
                right(at, j)

    with scope("out_wait"):
        for slot in range(width):
            for layer in range(2):
                block_ref = out_ref.at[slot, :, pl.ds(layer * half, half), :]
                pltpu.make_async_copy(block_ref, block_ref, o_recv.at[slot, layer]).wait()
    with scope("send_wait"):
        for copy, condition in pending:
            if condition is None:
                copy.wait_send()
            else:
                pl.when(condition)(copy.wait_send)


def spread(size, x_ref, o_ref, buffer, in_sem, out_sem):
    width, block, tiles = size
    rows = buffer.shape[2]
    steps = block // rows

    def inward(k):
        i, at = k // steps, k % steps
        return pltpu.make_async_copy(x_ref.at[:, i, pl.ds(at * rows, rows), :], buffer.at[k], in_sem.at[k])

    def outward(k, j, tile):
        return pltpu.make_async_copy(
            buffer.at[k, j, :, pl.ds(tile * LANES, LANES)],
            o_ref.at[pl.ds(k * rows, rows), tile * width + j, 0, :], out_sem.at[k, j, tile],
        )

    every = range(width * steps)
    for k in every:
        inward(k).start()
    for k in every:
        inward(k).wait()
        for j in range(width):
            for tile in range(tiles):
                outward(k, j, tile).start()
    for k in every:
        for j in range(width):
            for tile in range(tiles):
                outward(k, j, tile).wait()


def shards(matrix, transforms):
    width, block, _, half = matrix.shape
    pair_dev = width // 2
    order = 2 * block
    rows_n, cols_n = lax.axis_size("row"), lax.axis_size("col")
    tiles = half // LANES
    raw_shape = (width * block, width * tiles, 1, LANES)
    own = transforms[0]
    piece = own.shape[1]
    pieces = 2 * cols_n
    f32, bf16 = jnp.float32, jnp.bfloat16

    raw = matrix.reshape(width * block, width, tiles, LANES).transpose(0, 2, 1, 3).reshape(raw_shape)
    any_space = pl.BlockSpec(memory_space=pl.ANY)
    dma = pltpu.SemaphoreType.DMA
    vmem = pltpu.VMEM
    by_piece = (2, pair_dev)
    flops = 3 * 2 * 2 * width * half * order * width * block
    outs = pl.pallas_call(
        functools.partial(sweep, (rows_n, cols_n, pair_dev, width, block, half, piece)),
        name="sweep",
        out_shape=[
            jax.ShapeDtypeStruct((width, width, block, half), f32),
            jax.ShapeDtypeStruct(raw_shape, f32),
            jax.ShapeDtypeStruct((pair_dev, 2, order, half), f32),
            jax.ShapeDtypeStruct((pair_dev, 2, order, half), f32),
            jax.ShapeDtypeStruct((rows_n, 2, pair_dev, piece, block), f32),
            jax.ShapeDtypeStruct((pieces, 2, pair_dev, piece, block), f32),
            jax.ShapeDtypeStruct((width, width, half, block), f32),
            jax.ShapeDtypeStruct((2, 2, half, half), f32),
        ],
        in_specs=[any_space, any_space],
        out_specs=[any_space] * 8,
        scratch_shapes=[
            vmem((pair_dev, order, width * block), bf16),
            vmem((pair_dev, order, width * block), bf16),
            vmem((width, half, order), bf16),
            vmem((width, half, order), bf16),
            vmem((width, order, block), bf16),
            vmem((width, order, block), bf16),
            vmem((width, half, width * block), bf16),
            vmem((width, half, width * block), bf16),
            vmem((width * width, half, block), f32),
            vmem((width * width, half, block), f32),
            vmem((pair_dev, piece, order), f32),
            vmem((2, ROWS, width * half), f32),
            vmem((2, pair_dev, 2 * piece, half), f32),
            vmem((4, pair_dev, piece, block), f32),
            vmem((2, half, block), f32),
            dma((2,)), dma((4,)), dma((2,) + by_piece),
            dma((pair_dev,)), dma((pair_dev,)),
            dma((cols_n, 2) + by_piece), dma((cols_n, 2) + by_piece),
            dma((rows_n,) + by_piece), dma((rows_n,) + by_piece), dma((rows_n,) + by_piece), dma((rows_n,) + by_piece),
            dma((rows_n,) + by_piece), dma((rows_n,) + by_piece), dma((cols_n,) + by_piece),
            dma((cols_n, 2)), dma((cols_n, 2)), dma(by_piece), dma(by_piece),
            dma((width, width)), dma((width, width)),
            dma((width * width, 2)), dma((width, 2)),
            dma((2, 2)), dma((2, 2)),
        ],
        compiler_params=pltpu.CompilerParams(
            collective_id=0, has_side_effects=True, vmem_limit_bytes=VMEM_LIMIT
        ),
        cost_estimate=pl.CostEstimate(flops=flops, bytes_accessed=0, transcendentals=0),
    )(raw, own)
    blocks = outs[0]

    steps = width * block // ROWS
    result = pl.pallas_call(
        functools.partial(spread, (width, block, tiles)),
        name="spread",
        in_specs=[any_space],
        out_specs=any_space,
        out_shape=jax.ShapeDtypeStruct(raw_shape, f32),
        scratch_shapes=[
            vmem((steps, width, ROWS, half), f32), dma((steps,)), dma((steps, width, tiles)),
        ],
    )(blocks)
    result = result.reshape(width, block, tiles, width, LANES).transpose(0, 1, 3, 2, 4)
    return result.reshape(width, block, width, half)


def solution(mesh):
    return jax.shard_map(
        shards,
        mesh=mesh,
        in_specs=(P("row", None, "col", "layer"), P(None, "row", ("col", "layer"), None)),
        out_specs=P("row", None, "col", "layer"),
        check_vma=False,
    )
```

time: 214 us -> 173 us (0.81)
  the two profiles are of different devices: /device:TPU:5 before, /device:TPU:3 now
where the time goes in v1:
time: 173 us; the launch traced here: 172 us
  Pallas kernels  172 us (99%)
    pallas_call x1, Pallas kernels, shards(): pl.pallas_call(functools.partial(sweep, (rows_n, cols_n, pair_dev, width,...  165 us
    pallas_call x1, Pallas kernels, shards(): pl.pallas_call(functools.partial(spread, (width, block, tiles)), name='sp...  6.88 us

profile of v1, /device:TPU:3, one launch (start us, length us, event | category | flops | bytes accessed | tf_op | source)
XLA Modules:
  0.0 172.1 jit_solution(15143069048068928479)
XLA Ops:
  0.0 165.1 %sweep.1 = (f32[4,4,512,256]{3,2,1,0:T(8,128)}, f32[2048,8,1,128]{3,2,1,0:T(1,128)}, f32[2,2,1024,256]{3,2,1,0:T(8,128)}, f32[2,2,1024,256]{3,2,1,0:T(8,128)}, f...) custom-call(f32[2048,8,1,128]{3,2,1,0:T(1,128)} %bitcast.11, ...), custom_call_target="tpu_custom_call" | custom-call | flops 25769803776 | tf_op jit(solution)/shard_map/sweep/pallas_call | solution.py:617
  165.1 6.9 %spread.1 = f32[2048,8,1,128]{3,2,1,0:T(1,128)} custom-call(f32[4,4,512,256]{3,2,1,0:T(8,128)} %get-tuple-element.6.x_ref), custom_call_target="tpu_custom_call" | custom-call | tf_op jit(solution)/shard_map/spread/pallas_call | solution.py:666

commit v2 on v1

v2 whole, which is shorter than its diff:
```python
import functools

import jax
import jax.numpy as jnp
from jax import lax
from jax.experimental import pallas as pl
from jax.experimental.pallas import tpu as pltpu
from jax.sharding import PartitionSpec as P

MESH = pl.DeviceIdType.MESH
LANES = 128
ROWS = 256
VMEM_LIMIT = 66_000_000
scope = jax.named_scope


def halves_of(x):
    high = x.astype(jnp.bfloat16)
    low = (x - high.astype(jnp.float32)).astype(jnp.bfloat16)
    return high, low


def three_dots(a_high, a_low, b_high, b_low):
    def dot(a, b):
        return lax.dot_general(a, b, (((1,), (0,)), ((), ())), preferred_element_type=jnp.float32)

    return dot(a_high, b_high) + (dot(a_high, b_low) + dot(a_low, b_high))


def sweep(
    size,
    a_ref, t_ref,
    out_ref, ap_ref, jr_ref, jo_ref, z_ref, lr_ref, via_ref,
    a_hi, a_lo, jt_hi, jt_lo, jc_hi, jc_lo, lr_hi, lr_lo, l_tile, o_tile,
    own_v, a_stage, j_stage, l_stage,
    stage_sem, j_sem, own_sem,
    ap_send, ap_recv, jr_send, jr_recv,
    zo_send, zu_send, zu_recv, zd_send, zd_recv,
    ju_send, jd_send, jc_recv, jo_send, jo_recv,
    lr_send, lr_recv, o_send, o_recv, via_send, via_recv,
):
    rows_n, cols_n, pair_dev, width, block, half, piece = size
    order = 2 * block
    tiles = half // LANES
    r = lax.axis_index("row")
    c = lax.axis_index("col")
    l = lax.axis_index("layer")
    other = 1 - l
    partner = (r, c, other)
    mine = c * 2 + l
    square = cols_n == 4
    pending = []

    def remote(src, dst, send, recv, device):
        return pltpu.make_async_remote_copy(
            src_ref=src, dst_ref=dst, send_sem=send, recv_sem=recv, device_id=device, device_id_type=MESH
        )

    def send(copy, condition=None):
        if condition is None:
            copy.start()
        else:
            pl.when(condition)(copy.start)
        pending.append((copy, condition))

    def lanes(start, count):
        return pl.ds(pl.multiple_of(start, LANES), count)

    def member(s, p):
        return 1 - p if s == 0 else p

    def slot_of(s, p):
        return 2 * p + member(s, p)

    barrier = pltpu.get_barrier_semaphore()
    for mask in range(cols_n):
        for layer in (l, other):
            if mask == 0 and layer is l:
                continue
            pl.semaphore_signal(barrier, inc=1, device_id=(r, c ^ mask, layer), device_id_type=MESH)
    has_next = r + 1 < rows_n
    has_prev = r > 0

    for layer in (l, other):
        @pl.when(has_next)
        def _():
            pl.semaphore_signal(barrier, inc=1, device_id=(r + 1, c, layer), device_id_type=MESH)

        @pl.when(has_prev)
        def _():
            pl.semaphore_signal(barrier, inc=1, device_id=(r - 1, c, layer), device_id_type=MESH)

    with scope("barrier"):
        pl.semaphore_wait(barrier, 2 * (cols_n + has_next.astype(jnp.int32) + has_prev.astype(jnp.int32)) - 1)

    def part(m, layer):
        return lanes(m * block + layer * half, half)

    def plane_copy(mask, side, s, p, origin, source, device):
        m = member(s, p)
        dst = jr_ref.at[p, m, pl.ds(pl.multiple_of(origin * piece, piece), piece), :]
        return remote(source if source is not None else dst, dst, jr_send.at[mask, side, s, p],
                      jr_recv.at[mask, side, s, p], device)

    def plane_out(s, masks, pairs=range(pair_dev)):
        for mask in masks:
            for p in pairs:
                for side, layer in ((0, l), (1, other)):
                    if mask == 0 and side == 0:
                        continue
                    src = t_ref.at[p, :, part(member(s, p), layer)]
                    send(plane_copy(mask, side, s, p, mine, src, (r, c ^ mask, layer)))

    seen = set()

    def plane_wait(mask, s, p):
        if (mask, s, p) in seen:
            return
        seen.add((mask, s, p))
        for side, layer in ((0, l), (1, other)):
            if mask == 0 and side == 0:
                continue
            plane_copy(mask, side, s, p, (c ^ mask) * 2 + layer, None, partner).wait_recv()

    def plane_relay(s, p, mask):
        plane_wait(mask, s, p)
        for side, layer in ((0, l), (1, other)):
            send(plane_copy(3, side, s, p, (c ^ mask) * 2 + layer, None, (r, c ^ mask ^ 3, l)))

    same = r == c
    differs = r != c
    wide = 2 * piece

    def chip_rows(column):
        return pl.ds(pl.multiple_of(column * wide, wide), wide)

    def left_unit(mask, s, p):
        return jr_ref.at[p, member(s, p), chip_rows(c ^ mask), :]

    def handed(mask, s, p, src):
        return remote(
            src, jo_ref.at[mask, s, p], jo_send.at[mask, s, p], jo_recv.at[mask, s, p], partner
        )

    def halves_out(s):
        for mask in range(cols_n):
            for p in range(pair_dev):
                send(handed(mask, s, p, left_unit(mask, s, p)), same)

    kinds = (0, 1) if square else (0,)

    def carried(kind, s, group, up):
        if not square:
            return True
        side = ((c ^ group) & 1) == 0
        if s == 1:
            return side
        crossed = (group == 1) if up else (group == rows_n - 2)
        return crossed & side if kind else jnp.logical_not(crossed) | side

    def ways():
        return (
            (True, has_next, r + 1, zu_send, zu_recv), (False, has_prev, r - 1, zd_send, zd_recv)
        )

    def rows_out(s):
        for p in range(pair_dev):
            for side, layer in ((0, l), (1, other)):
                for up, there, to, _, recv in ways():
                    send(remote(
                        t_ref.at[p, :, part(member(s, p), layer)],
                        z_ref.at[r, 0, s, p, pl.ds(pl.multiple_of(l * piece, piece), piece), :],
                        zo_send.at[int(up), side, s, p], recv.at[1, 0, s, p], (to, c, layer),
                    ), there & carried(0, s, r, up))

    def rows_across(s):
        for p in range(pair_dev):
            plane_wait(1, s, p)
            for up, there, to, snd, recv in ways():
                send(remote(
                    left_unit(1, s, p), z_ref.at[r, 1, s, p], snd.at[0, 1, s, p], recv.at[1, 1, s, p], (to, c, l)
                ), there & carried(1, s, r, up))

    def arrivals(s, step):
        for kind in kinds:
            for up, recv, snd, plane, to, into in (
                (True, zu_recv, zu_send, r - step, r + 1, ju_send),
                (False, zd_recv, zd_send, r + step, r - 1, jd_send),
            ):
                at = jnp.clip(plane, 0, rows_n - 1)
                here = (plane >= 0) & (plane < rows_n) & carried(kind, s, at, up)
                onward = here & (to >= 0) & (to < rows_n)
                yield kind, recv, snd, at, here, onward, to, into

    def hand_over(s, step, among, only=None, ends=None):
        for p in range(pair_dev):
            for kind, _, _, at, here, onward, _, into in arrivals(s, step):
                if only not in (None, kind):
                    continue
                chosen = (onward if among else here & jnp.logical_not(onward)) & (at != c)
                if ends is not None:
                    at_end = (at == 0) | (at == rows_n - 1)
                    chosen = chosen & (at_end if ends else jnp.logical_not(at_end))
                mask = (c ^ at) ^ kind
                send(remote(
                    z_ref.at[at, kind, s, p], z_ref.at[at, mask, s, p], into.at[step, kind, s, p],
                    jc_recv.at[mask, s, p], (r, at, l),
                ), chosen)

    def forward(s, step, give=True, only=None, ends=None):
        for p in range(pair_dev):
            for kind, recv, snd, at, _, onward, to, _ in arrivals(s, step):
                block_ref = z_ref.at[at, kind, s, p]
                if step + 1 == rows_n or only not in (None, kind):
                    continue
                if ends is not None:
                    at_end = (at == 0) | (at == rows_n - 1)
                    onward = onward & (at_end if ends else jnp.logical_not(at_end))

                @pl.when(onward)
                def _():
                    remote(block_ref, block_ref, snd.at[step, kind, s, p], recv.at[step, kind, s, p],
                           partner).wait_recv()

                send(remote(
                    block_ref, block_ref, snd.at[step, kind, s, p], recv.at[step + 1, kind, s, p], (to, c, l)
                ), onward)
        if give:
            hand_over(s, step, True, only, ends)

    def finish(s, step):
        for p in range(pair_dev):
            for kind, recv, snd, at, here, onward, _, _ in arrivals(s, step):
                block_ref = z_ref.at[at, kind, s, p]

                @pl.when(here & jnp.logical_not(onward))
                def _():
                    remote(block_ref, block_ref, snd.at[step, kind, s, p], recv.at[step, kind, s, p],
                           partner).wait_recv()

        hand_over(s, step, False)

    def columns_copy(p):
        rows = pl.ds(p * order, order)
        return remote(a_ref.at[rows], ap_ref.at[rows], ap_send.at[p], ap_recv.at[p], partner)

    def split_columns(src, layer, p):
        count = order // ROWS

        def fetch(at):
            slot = lax.rem(at, 2)
            rows = pl.ds(pl.multiple_of(p * order + at * ROWS, ROWS), ROWS)
            for j in range(width):
                for tile in range(tiles):
                    pltpu.make_async_copy(
                        src.at[rows, tile * width + j, 0, :],
                        a_stage.at[slot, :, pl.ds(j * half + tile * LANES, LANES)],
                        stage_sem.at[slot],
                    ).start()

        def body(at, carry):
            @pl.when(at + 1 < count)
            def _():
                fetch(at + 1)

            slot = lax.rem(at, 2)
            pltpu.make_async_copy(a_stage.at[slot], a_stage.at[slot], stage_sem.at[slot]).wait()
            rows = pl.ds(pl.multiple_of(at * ROWS, ROWS), ROWS)
            for j in range(width):
                high, low = halves_of(a_stage[slot, :, j * half : (j + 1) * half])
                cols = lanes(j * block + layer * half, half)
                a_hi[p, rows, cols] = high
                a_lo[p, rows, cols] = low
            return carry

        fetch(0)
        lax.fori_loop(0, count, body, 0)

    def turn(s):
        def fetch(mask):
            for p in range(pair_dev):
                plane_wait(mask, s, p)
            for p in range(pair_dev):
                pltpu.make_async_copy(left_unit(mask, s, p), j_stage.at[mask % 2, p], j_sem.at[mask % 2]).start()

        fetch(0)
        for mask in range(cols_n):
            if mask + 1 < cols_n:
                fetch(mask + 1)
            stage = j_stage.at[mask % 2]
            pltpu.make_async_copy(stage, stage, j_sem.at[mask % 2]).wait()
            at = lanes((c ^ mask) * wide, wide)
            for p in range(pair_dev):
                high, low = halves_of(j_stage[mask % 2, p].T)
                jt_hi[slot_of(s, p), :, at] = high
                jt_lo[slot_of(s, p), :, at] = low
        halves_out(s)

    def left(slot):
        p = slot // 2
        kept = slot in (0, width - 1)
        at = (jnp.where(has_prev, 2, 0) if slot == 0 else 1) if kept else None

        def body(n, carry):
            cols = lanes(n * block, block)
            x = three_dots(jt_hi[slot], jt_lo[slot], a_hi[p, :, cols], a_lo[p, :, cols])
            if kept:
                high, low = halves_of(x)
                lr_hi[at, :, cols] = high
                lr_lo[at, :, cols] = low
            else:
                l_tile[(slot - 1) * width + n] = x
            return carry

        lax.fori_loop(0, width, body, 0)

    def left_out(slot, order_of_tiles):
        if slot == 1:
            moved, target, at = has_prev, r - 1, jnp.where(has_prev, 3, 2)
        else:
            moved, target, at = has_next, r + 1, jnp.where(has_next, 0, 3)
        for n in order_of_tiles:
            src, dst = l_tile.at[(slot - 1) * width + n], lr_ref.at[at, n]
            send(remote(src, dst, lr_send.at[slot, n], lr_recv.at[at, n], (target, c, l)), moved)
            pl.when(jnp.logical_not(moved))(pltpu.make_async_copy(src, dst, lr_recv.at[at, n]).start)

    def right_pieces(s):
        deep = j_stage.shape[0]
        for mask in range(cols_n):
            for p in range(pair_dev):
                unit = z_ref.at[c, mask, s, p]
                late = differs
                if square and mask == 1:
                    late = differs & jnp.logical_not(jnp.where(r > c, c == 1, c == rows_n - 2))
                if mask and not (square and mask == 1 and s == 1):
                    @pl.when(late)
                    def _():
                        remote(unit, unit, jo_send.at[mask, s, p], jc_recv.at[mask, s, p], partner).wait_recv()

                send(handed(mask, s, p, unit), differs)
        jobs = [(side, mask) for side in range(2) for mask in range(cols_n)]

        def fetch(k):
            side, mask = jobs[k]
            for p in range(pair_dev):
                def take(src):
                    return pltpu.make_async_copy(src, j_stage.at[k % deep, p], j_sem.at[k % deep])

                if side:
                    src = jo_ref.at[mask, s, p]
                    handed(mask, s, p, src).wait_recv()
                    take(src).start()
                else:
                    pl.when(differs)(take(z_ref.at[c, mask, s, p]).start)
                    pl.when(same)(take(left_unit(mask, s, p)).start)

        for k in range(deep - 1):
            fetch(k)
        for k, (side, mask) in enumerate(jobs):
            if k + deep - 1 < len(jobs):
                fetch(k + deep - 1)
            stage = j_stage.at[k % deep]
            pltpu.make_async_copy(stage, stage, j_sem.at[k % deep]).wait()
            cols = lanes((other if side else l) * half, half)
            for p in range(pair_dev):
                high, low = halves_of(j_stage[k % deep, p])
                jc_hi[slot_of(s, p), chip_rows(c ^ mask), cols] = high
                jc_lo[slot_of(s, p), chip_rows(c ^ mask), cols] = low

    def left_rows(at, q):
        loads = []
        for n in range(2):
            src = lr_ref.at[at, 2 * q + n]
            pltpu.make_async_copy(src, src, lr_recv.at[at, 2 * q + n]).wait()
            loads.append(pltpu.make_async_copy(src, l_stage.at[n], stage_sem.at[n]))
            loads[-1].start()
        for n in range(2):
            loads[n].wait()
            high, low = halves_of(l_stage[n])
            cols = lanes((2 * q + n) * block, block)
            lr_hi[at, :, cols] = high
            lr_lo[at, :, cols] = low

    left_end, right_end = c > 0, c + 1 < cols_n
    staying, arriving = (1, width - 2), (0, width - 1)
    by_way = staying if square else ()
    low_rows = pl.ds(pl.multiple_of(l * half, half), half)

    def right_tile(at, j, q):
        rows = lanes(q * order, order)
        tile = at * width + j
        o_tile[tile] = three_dots(lr_hi[at, :, rows], lr_lo[at, :, rows], jc_hi[j], jc_lo[j])
        return tile

    def right_moving(at, q):
        j = 1 + q
        tile = right_tile(at, j, q)
        up = q == 1
        moved = jnp.where(up, right_end, left_end)
        target = jnp.where(up, c + 1, c - 1)
        slot = jnp.where(up, jnp.where(right_end, 0, 3), jnp.where(left_end, 3, 2))
        column = jnp.where(moved, target, c)
        dst = out_ref.at[slot, at, low_rows, :]
        around = None
        if isinstance(at, int) and at in by_way:
            around = jnp.where(up, c == 1, c == 2)
        for s, layer in ((0, l), (1, other)):
            src = o_tile.at[tile, :, lanes(layer * half, half)]
            condition = moved if s == 0 else None
            if around is not None:
                index = by_way.index(at)
                send(remote(
                    src, via_ref.at[index, l], o_send.at[tile, s], via_recv.at[index, l], (r, c ^ 2, layer)
                ), around)
                direct = jnp.logical_not(around)
                condition = direct if condition is None else condition & direct
            send(remote(src, dst, o_send.at[tile, s], o_recv.at[slot, l], (r, column, layer)), condition)
            if s == 0:
                pl.when(jnp.logical_not(moved))(pltpu.make_async_copy(src, dst, o_recv.at[slot, l]).start)

    def right_kept(at, j):
        tile = right_tile(at, j, j // 2)
        slot = jnp.where(left_end, 2, 0) if j == 0 else 1
        dst = out_ref.at[slot, at, low_rows, :]
        send(remote(
            o_tile.at[tile, :, lanes(other * half, half)], dst, o_send.at[tile, 1], o_recv.at[slot, l], partner
        ))
        pltpu.make_async_copy(
            o_tile.at[tile, :, lanes(l * half, half)], dst, o_recv.at[slot, l]
        ).start()

    def right_relay(index):
        outer = (c == 0) | (c == cols_n - 1)
        slot = jnp.where(c == 0, 3, 0)
        for layer in range(2):
            src = via_ref.at[index, layer]
            rows = pl.ds(layer * half, half)

            @pl.when(outer)
            def _():
                remote(src, src, via_send.at[index, layer], via_recv.at[index, layer], partner).wait_recv()

            send(remote(
                src, out_ref.at[slot, by_way[index], rows, :], via_send.at[index, layer], o_recv.at[slot, layer],
                (r, c ^ 1, l),
            ), outer)

    rows_out(0)
    if square:
        plane_out(0, (1, 2, 0))
        plane_out(1, (1, 0))
    else:
        for s in range(2):
            plane_out(s, list(range(1, cols_n)) + [0])
    for p in range(pair_dev):
        send(columns_copy(p))
    load = pltpu.make_async_copy(t_ref, own_v, own_sem.at[0, 0, 0])
    load.start()
    load.wait()
    fills = []
    for s in range(2):
        for p in range(pair_dev):
            fills.append(pltpu.make_async_copy(
                own_v.at[p, :, part(member(s, p), l)],
                jr_ref.at[p, member(s, p), pl.ds(pl.multiple_of(mine * piece, piece), piece), :],
                own_sem.at[1, s, p],
            ))
    for copy in fills:
        copy.start()
    with scope("split_own"):
        for p in range(pair_dev):
            split_columns(a_ref, l, p)
    for copy in fills:
        copy.wait()
    if square:
        with scope("relay0"):
            for p in range(pair_dev):
                plane_relay(0, p, 1)
        plane_out(1, (2,))
        rows_across(0)
    with scope("fwd_a1"):
        forward(0, 1, only=0)
    rows_out(1)
    with scope("split_p0"):
        columns_copy(0).wait_recv()
        split_columns(ap_ref, other, 0)
    with scope("split_p1"):
        for p in range(1, pair_dev):
            columns_copy(p).wait_recv()
            split_columns(ap_ref, other, p)
    if square:
        with scope("fwd_a1x"):
            forward(0, 1, only=1)
        with scope("across1"):
            rows_across(1)
    with scope("fwd_b1e0"):
        forward(1, 1, only=0, ends=True)
    with scope("turn_a"):
        turn(0)
    with scope("left_a2"):
        left(width - 2)
    for step in range(2, rows_n - 1):
        with scope("fwd_a2"):
            forward(0, step, False)
    if square:
        with scope("fwd_b1e"):
            forward(1, 1, only=1, ends=True)
    with scope("left_a1"):
        left(1)
    if square:
        with scope("relay1"):
            for p in range(pair_dev):
                plane_relay(1, p, 2)
    for step in range(2, rows_n - 1):
        hand_over(0, step, True)
    for step in range(1, rows_n):
        with scope("fin_a"):
            finish(0, step)
    for step in range(2, rows_n - 1):
        with scope("fwd_b2"):
            forward(1, step)
    with scope("turn_b"):
        turn(1)
    with scope("left_b"):
        for slot in (0, width - 1):
            left(slot)
    with scope("fwd_b1m"):
        forward(1, 1, ends=False)
    first, last = (0, 1), (2, 3)
    for tiles_first, tiles_last in ((first, last), (last, first)):
        left_out(width - 2, tiles_first)
        left_out(1, tiles_last)
    with scope("rows"):
        @pl.when(jnp.logical_not(has_prev))
        def _():
            for q in range(pair_dev):
                left_rows(2, q)
    with scope("pieces_a"):
        right_pieces(0)
    for at in staying:
        with scope("right"):
            for q in range(pair_dev):
                right_moving(at, q)

    first, last = jnp.logical_not(has_prev), jnp.logical_not(has_next)

    def arrived(at, q):
        with scope("rows_arr"):
            @pl.when(has_prev | (at == width - 1))
            def _():
                left_rows(at, q)
        with scope("right"):
            right_moving(at, q)

    top, low = 0, width - 1
    arrived(jnp.where(last, low, top), jnp.where(last, 1, 0))
    arrived(jnp.where(first, top, low), jnp.where(last, 0, 1))
    for step in range(1, rows_n):
        with scope("fin_b"):
            finish(1, step)
    if square:
        with scope("via0"):
            right_relay(0)
            right_relay(1)
    arrived(jnp.where(first, low, top), jnp.where(last, 0, 1))
    arrived(jnp.where(last, top, low), jnp.where(last, 1, 0))
    with scope("pieces_b"):
        right_pieces(1)
    with scope("right_local"):
        for at in staying + arriving:
            for j in (0, width - 1):
                right_kept(at, j)

    with scope("out_wait"):
        for slot in range(width):
            for layer in range(2):
                block_ref = out_ref.at[slot, :, pl.ds(layer * half, half), :]
                pltpu.make_async_copy(block_ref, block_ref, o_recv.at[slot, layer]).wait()
    with scope("send_wait"):
        for copy, condition in pending:
            if condition is None:
                copy.wait_send()
            else:
                pl.when(condition)(copy.wait_send)


def spread(size, x_ref, o_ref, buffer, in_sem, out_sem):
    width, block, tiles = size
    rows = buffer.shape[2]
    steps = block // rows

    def inward(k):
        i, at = k // steps, k % steps
        return pltpu.make_async_copy(x_ref.at[:, i, pl.ds(at * rows, rows), :], buffer.at[k], in_sem.at[k])

    def outward(k, j, tile):
        return pltpu.make_async_copy(
            buffer.at[k, j, :, pl.ds(tile * LANES, LANES)],
            o_ref.at[pl.ds(k * rows, rows), tile * width + j, 0, :], out_sem.at[k, j, tile],
        )

    every = range(width * steps)
    for k in every:
        inward(k).start()
    for k in every:
        inward(k).wait()
        for j in range(width):
            for tile in range(tiles):
                outward(k, j, tile).start()
    for k in every:
        for j in range(width):
            for tile in range(tiles):
                outward(k, j, tile).wait()


def shards(matrix, transforms):
    width, block, _, half = matrix.shape
    pair_dev = width // 2
    order = 2 * block
    rows_n, cols_n = lax.axis_size("row"), lax.axis_size("col")
    tiles = half // LANES
    raw_shape = (width * block, width * tiles, 1, LANES)
    own = transforms[0]
    piece = own.shape[1]
    f32, bf16 = jnp.float32, jnp.bfloat16

    raw = matrix.reshape(width * block, width, tiles, LANES).transpose(0, 2, 1, 3).reshape(raw_shape)
    any_space = pl.BlockSpec(memory_space=pl.ANY)
    dma = pltpu.SemaphoreType.DMA
    vmem = pltpu.VMEM
    by_piece = (2, pair_dev)
    by_unit = by_piece + (2 * piece, half)
    flops = 3 * 2 * 2 * width * half * order * width * block
    outs = pl.pallas_call(
        functools.partial(sweep, (rows_n, cols_n, pair_dev, width, block, half, piece)),
        name="sweep",
        out_shape=[
            jax.ShapeDtypeStruct((width, width, block, half), f32),
            jax.ShapeDtypeStruct(raw_shape, f32),
            jax.ShapeDtypeStruct((pair_dev, 2, order, half), f32),
            jax.ShapeDtypeStruct((cols_n,) + by_unit, f32),
            jax.ShapeDtypeStruct((rows_n, cols_n) + by_unit, f32),
            jax.ShapeDtypeStruct((width, width, half, block), f32),
            jax.ShapeDtypeStruct((2, 2, half, half), f32),
        ],
        in_specs=[any_space, any_space],
        out_specs=[any_space] * 7,
        scratch_shapes=[
            vmem((pair_dev, order, width * block), bf16),
            vmem((pair_dev, order, width * block), bf16),
            vmem((width, half, order), bf16),
            vmem((width, half, order), bf16),
            vmem((width, order, block), bf16),
            vmem((width, order, block), bf16),
            vmem((width, half, width * block), bf16),
            vmem((width, half, width * block), bf16),
            vmem((2 * width, half, block), f32),
            vmem((width * width, half, block), f32),
            vmem((pair_dev, piece, order), f32),
            vmem((2, ROWS, width * half), f32),
            vmem((4, pair_dev, 2 * piece, half), f32),
            vmem((2, half, block), f32),
            dma((2,)), dma((4,)), dma((2,) + by_piece),
            dma((pair_dev,)), dma((pair_dev,)),
            dma((cols_n, 2) + by_piece), dma((cols_n, 2) + by_piece),
            dma((2, 2) + by_piece),
            dma((rows_n, 2) + by_piece), dma((rows_n, 2) + by_piece),
            dma((rows_n, 2) + by_piece), dma((rows_n, 2) + by_piece),
            dma((rows_n, 2) + by_piece), dma((rows_n, 2) + by_piece), dma((cols_n,) + by_piece),
            dma((cols_n,) + by_piece), dma((cols_n,) + by_piece),
            dma((width, width)), dma((width, width)),
            dma((width * width, 2)), dma((width, 2)),
            dma((2, 2)), dma((2, 2)),
        ],
        compiler_params=pltpu.CompilerParams(
            collective_id=0, has_side_effects=True, vmem_limit_bytes=VMEM_LIMIT
        ),
        cost_estimate=pl.CostEstimate(flops=flops, bytes_accessed=0, transcendentals=0),
    )(raw, own)
    blocks = outs[0]

    steps = width * block // ROWS
    result = pl.pallas_call(
        functools.partial(spread, (width, block, tiles)),
        name="spread",
        in_specs=[any_space],
        out_specs=any_space,
        out_shape=jax.ShapeDtypeStruct(raw_shape, f32),
        scratch_shapes=[
            vmem((steps, width, ROWS, half), f32), dma((steps,)), dma((steps, width, tiles)),
        ],
    )(blocks)
    result = result.reshape(width, block, tiles, width, LANES).transpose(0, 1, 3, 2, 4)
    return result.reshape(width, block, width, half)


def solution(mesh):
    return jax.shard_map(
        shards,
        mesh=mesh,
        in_specs=(P("row", None, "col", "layer"), P(None, "row", ("col", "layer"), None)),
        out_specs=P("row", None, "col", "layer"),
        check_vma=False,
    )
```

time: 173 us -> 163 us (0.942)
  the two profiles are of different devices: /device:TPU:3 before, /device:TPU:5 now
where the time goes in v2:
time: 163 us; the launch traced here: 162 us
  Pallas kernels  162 us (99%)
    pallas_call x1, Pallas kernels, shards(): pl.pallas_call(functools.partial(sweep, (rows_n, cols_n, pair_dev, width,...  155 us
    pallas_call x1, Pallas kernels, shards(): pl.pallas_call(functools.partial(spread, (width, block, tiles)), name='sp...  6.88 us

profile of v2, /device:TPU:5, one launch (start us, length us, event | category | flops | bytes accessed | tf_op | source)
XLA Modules:
  0.0 162.5 jit_solution(17264546915881642908)
XLA Ops:
  0.0 155.4 %sweep.1 = (f32[4,4,512,256]{3,2,1,0:T(8,128)}, f32[2048,8,1,128]{3,2,1,0:T(1,128)}, f32[2,2,1024,256]{3,2,1,0:T(8,128)}, f32[4,2,2,256,256]{4,3,2,1,0:T(8,128)}...) custom-call(f32[2048,8,1,128]{3,2,1,0:T(1,128)} %bitcast.11, ...), custom_call_target="tpu_custom_call" | custom-call | flops 25769803776 | tf_op jit(solution)/shard_map/sweep/pallas_call | solution.py:634
  155.4 6.9 %spread.1 = f32[2048,8,1,128]{3,2,1,0:T(1,128)} custom-call(f32[4,4,512,256]{3,2,1,0:T(8,128)} %get-tuple-element.6.x_ref), custom_call_target="tpu_custom_call" | custom-call | tf_op jit(solution)/shard_map/spread/pallas_call | solution.py:683

commit v3 on v2

--- a/solution.py
+++ b/solution.py
@@ -69,6 +69,9 @@
     def member(s, p):
         return 1 - p if s == 0 else p
 
+    def leading(group, k):
+        return jnp.where((group & 1) == 0 if square else group == 0, 1 - k, k)
+
     def slot_of(s, p):
         return 2 * p + member(s, p)
 
@@ -164,7 +167,8 @@
         )
 
     def rows_out(s):
-        for p in range(pair_dev):
+        for k in range(pair_dev):
+            p = leading(r, k)
             for side, layer in ((0, l), (1, other)):
                 for up, there, to, _, recv in ways():
                     send(remote(
@@ -173,13 +177,15 @@
                         zo_send.at[int(up), side, s, p], recv.at[1, 0, s, p], (to, c, layer),
                     ), there & carried(0, s, r, up))
 
-    def rows_across(s):
+    def rows_across(s, among=True):
         for p in range(pair_dev):
             plane_wait(1, s, p)
+        for k in range(pair_dev):
+            p = leading(r, k)
             for up, there, to, snd, recv in ways():
                 send(remote(
                     left_unit(1, s, p), z_ref.at[r, 1, s, p], snd.at[0, 1, s, p], recv.at[1, 1, s, p], (to, c, l)
-                ), there & carried(1, s, r, up))
+                ), there & among & carried(1, s, r, up))
 
     def arrivals(s, step):
         for kind in kinds:
@@ -192,12 +198,15 @@
                 onward = here & (to >= 0) & (to < rows_n)
                 yield kind, recv, snd, at, here, onward, to, into
 
-    def hand_over(s, step, among, only=None, ends=None):
-        for p in range(pair_dev):
+    def hand_over(s, step, among, only=None, ends=None, near=None):
+        for k in range(pair_dev):
             for kind, _, _, at, here, onward, _, into in arrivals(s, step):
+                p = leading(at, k)
                 if only not in (None, kind):
                     continue
                 chosen = (onward if among else here & jnp.logical_not(onward)) & (at != c)
+                if near is not None:
+                    chosen = chosen & ((at == (c ^ 1)) if near else (at != (c ^ 1)))
                 if ends is not None:
                     at_end = (at == 0) | (at == rows_n - 1)
                     chosen = chosen & (at_end if ends else jnp.logical_not(at_end))
@@ -207,9 +216,13 @@
                     jc_recv.at[mask, s, p], (r, at, l),
                 ), chosen)
 
-    def forward(s, step, give=True, only=None, ends=None):
-        for p in range(pair_dev):
+    def forward(s, step, give=True, only=None, ends=None, clear=None):
+        for k in range(pair_dev):
             for kind, recv, snd, at, _, onward, to, _ in arrivals(s, step):
+                p = leading(at, k)
+                if clear is not None:
+                    busy = ((c ^ jnp.where(to > r, 1, rows_n - 2)) & 1) == 0
+                    onward = onward & (jnp.logical_not(busy) if clear else busy)
                 block_ref = z_ref.at[at, kind, s, p]
                 if step + 1 == rows_n or only not in (None, kind):
                     continue
@@ -228,9 +241,10 @@
         if give:
             hand_over(s, step, True, only, ends)
 
-    def finish(s, step):
-        for p in range(pair_dev):
+    def finish(s, step, near=None):
+        for k in range(pair_dev):
             for kind, recv, snd, at, here, onward, _, _ in arrivals(s, step):
+                p = leading(at, k)
                 block_ref = z_ref.at[at, kind, s, p]
 
                 @pl.when(here & jnp.logical_not(onward))
@@ -238,7 +252,7 @@
                     remote(block_ref, block_ref, snd.at[step, kind, s, p], recv.at[step, kind, s, p],
                            partner).wait_recv()
 
-        hand_over(s, step, False)
+        hand_over(s, step, False, near=near)
 
     def columns_copy(p):
         rows = pl.ds(p * order, order)
@@ -324,48 +338,51 @@
             send(remote(src, dst, lr_send.at[slot, n], lr_recv.at[at, n], (target, c, l)), moved)
             pl.when(jnp.logical_not(moved))(pltpu.make_async_copy(src, dst, lr_recv.at[at, n]).start)
 
-    def right_pieces(s):
-        deep = j_stage.shape[0]
+    def right_pieces(s, p):
+        depth = j_stage.shape[0] * pair_dev
         for mask in range(cols_n):
-            for p in range(pair_dev):
-                unit = z_ref.at[c, mask, s, p]
-                late = differs
-                if square and mask == 1:
-                    late = differs & jnp.logical_not(jnp.where(r > c, c == 1, c == rows_n - 2))
-                if mask and not (square and mask == 1 and s == 1):
-                    @pl.when(late)
-                    def _():
-                        remote(unit, unit, jo_send.at[mask, s, p], jc_recv.at[mask, s, p], partner).wait_recv()
-
-                send(handed(mask, s, p, unit), differs)
+            unit = z_ref.at[c, mask, s, p]
+            late = differs
+            if square and mask == 1:
+                late = differs & jnp.logical_not(jnp.where(r > c, c == 1, c == rows_n - 2))
+            if mask and not (square and mask == 1 and s == 1):
+                @pl.when(late)
+                def _():
+                    remote(unit, unit, jo_send.at[mask, s, p], jc_recv.at[mask, s, p], partner).wait_recv()
+
+            send(handed(mask, s, p, unit), differs)
         jobs = [(side, mask) for side in range(2) for mask in range(cols_n)]
+
+        def place(k):
+            at = k % depth
+            return j_stage.at[at // pair_dev, at % pair_dev], j_sem.at[at]
 
         def fetch(k):
             side, mask = jobs[k]
-            for p in range(pair_dev):
-                def take(src):
-                    return pltpu.make_async_copy(src, j_stage.at[k % deep, p], j_sem.at[k % deep])
-
-                if side:
-                    src = jo_ref.at[mask, s, p]
-                    handed(mask, s, p, src).wait_recv()
-                    take(src).start()
-                else:
-                    pl.when(differs)(take(z_ref.at[c, mask, s, p]).start)
-                    pl.when(same)(take(left_unit(mask, s, p)).start)
-
-        for k in range(deep - 1):
+
+            def take(src):
+                return pltpu.make_async_copy(src, *place(k))
+
+            if side:
+                src = jo_ref.at[mask, s, p]
+                handed(mask, s, p, src).wait_recv()
+                take(src).start()
+            else:
+                pl.when(differs)(take(z_ref.at[c, mask, s, p]).start)
+                pl.when(same)(take(left_unit(mask, s, p)).start)
+
+        ahead = depth - 1
+        for k in range(min(ahead, len(jobs))):
             fetch(k)
         for k, (side, mask) in enumerate(jobs):
-            if k + deep - 1 < len(jobs):
-                fetch(k + deep - 1)
-            stage = j_stage.at[k % deep]
-            pltpu.make_async_copy(stage, stage, j_sem.at[k % deep]).wait()
+            if k + ahead < len(jobs):
+                fetch(k + ahead)
+            stage, sem = place(k)
+            pltpu.make_async_copy(stage, stage, sem).wait()
             cols = lanes((other if side else l) * half, half)
-            for p in range(pair_dev):
-                high, low = halves_of(j_stage[k % deep, p])
-                jc_hi[slot_of(s, p), chip_rows(c ^ mask), cols] = high
-                jc_lo[slot_of(s, p), chip_rows(c ^ mask), cols] = low
+            high, low = halves_of(stage[...])
+            jc_hi[slot_of(s, p), chip_rows(c ^ mask), cols] = high
+            jc_lo[slot_of(s, p), chip_rows(c ^ mask), cols] = low
 
     def left_rows(at, q):
         loads = []
@@ -491,18 +508,26 @@
     if square:
         with scope("fwd_a1x"):
             forward(0, 1, only=1)
+        at_end = jnp.logical_not(has_prev & has_next)
         with scope("across1"):
-            rows_across(1)
+            rows_across(1, at_end)
+    with scope("fin_a1"):
+        finish(0, 1, near=True)
     with scope("fwd_b1e0"):
         forward(1, 1, only=0, ends=True)
+    if square:
+        for step in range(2, rows_n - 1):
+            with scope("fwd_a2c"):
+                forward(0, step, False, clear=True)
     with scope("turn_a"):
         turn(0)
     with scope("left_a2"):
         left(width - 2)
     for step in range(2, rows_n - 1):
         with scope("fwd_a2"):
-            forward(0, step, False)
+            forward(0, step, False, clear=False if square else None)
     if square:
+        rows_across(1, jnp.logical_not(at_end))
         with scope("fwd_b1e"):
             forward(1, 1, only=1, ends=True)
     with scope("left_a1"):
@@ -513,19 +538,23 @@
                 plane_relay(1, p, 2)
     for step in range(2, rows_n - 1):
         hand_over(0, step, True)
-    for step in range(1, rows_n):
+    hand_over(0, 1, False, near=False)
+    for step in range(2, rows_n):
         with scope("fin_a"):
             finish(0, step)
     for step in range(2, rows_n - 1):
         with scope("fwd_b2"):
             forward(1, step)
+    with scope("fwd_b1m0"):
+        forward(1, 1, only=0, ends=False)
     with scope("turn_b"):
         turn(1)
     with scope("left_b"):
-        for slot in (0, width - 1):
+        for slot in (width - 1, 0):
             left(slot)
-    with scope("fwd_b1m"):
-        forward(1, 1, ends=False)
+    if square:
+        with scope("fwd_b1m"):
+            forward(1, 1, only=1, ends=False)
     first, last = (0, 1), (2, 3)
     for tiles_first, tiles_last in ((first, last), (last, first)):
         left_out(width - 2, tiles_first)
@@ -535,11 +564,12 @@
         def _():
             for q in range(pair_dev):
                 left_rows(2, q)
-    with scope("pieces_a"):
-        right_pieces(0)
-    for at in staying:
+    for k in range(pair_dev):
+        q = leading(c, k)
+        with scope("pieces_a"):
+            right_pieces(0, q)
         with scope("right"):
-            for q in range(pair_dev):
+            for at in staying:
                 right_moving(at, q)
 
     first, last = jnp.logical_not(has_prev), jnp.logical_not(has_next)
@@ -565,7 +595,8 @@
     arrived(jnp.where(first, low, top), jnp.where(last, 0, 1))
     arrived(jnp.where(last, top, low), jnp.where(last, 1, 0))
     with scope("pieces_b"):
-        right_pieces(1)
+        for p in range(pair_dev):
+            right_pieces(1, p)
     with scope("right_local"):
         for at in staying + arriving:
             for j in (0, width - 1):
@@ -660,7 +691,7 @@
             vmem((2, ROWS, width * half), f32),
             vmem((4, pair_dev, 2 * piece, half), f32),
             vmem((2, half, block), f32),
-            dma((2,)), dma((4,)), dma((2,) + by_piece),
+            dma((2,)), dma((4 * pair_dev,)), dma((2,) + by_piece),
             dma((pair_dev,)), dma((pair_dev,)),
             dma((cols_n, 2) + by_piece), dma((cols_n, 2) + by_piece),
             dma((2, 2) + by_piece),

time: 163 us -> 154 us (0.945)
  Pallas kernels: 162 us -> 153 us
    pallas_call x1, Pallas kernels: 155 us -> 146 us  [shards(): pl.pallas_call(functools.partial(sweep, (rows_n, cols_n, pair_dev, width,...]
where the time goes in v3:
time: 154 us; the launch traced here: 153 us
  Pallas kernels  153 us (99%)
    pallas_call x1, Pallas kernels, shards(): pl.pallas_call(functools.partial(sweep, (rows_n, cols_n, pair_dev, width,...  146 us
    pallas_call x1, Pallas kernels, shards(): pl.pallas_call(functools.partial(spread, (width, block, tiles)), name='sp...  6.88 us

profile of v3, /device:TPU:5, one launch (start us, length us, event | category | flops | bytes accessed | tf_op | source)
XLA Modules:
  0.0 153.3 jit_solution(10544411896112607835)
XLA Ops:
  0.0 146.3 %sweep.1 = (f32[4,4,512,256]{3,2,1,0:T(8,128)}, f32[2048,8,1,128]{3,2,1,0:T(1,128)}, f32[2,2,1024,256]{3,2,1,0:T(8,128)}, f32[4,2,2,256,256]{4,3,2,1,0:T(8,128)}...) custom-call(f32[2048,8,1,128]{3,2,1,0:T(1,128)} %bitcast.11, ...), custom_call_target="tpu_custom_call" | custom-call | flops 25769803776 | tf_op jit(solution)/shard_map/sweep/pallas_call | solution.py:665
  146.3 6.9 %spread.1 = f32[2048,8,1,128]{3,2,1,0:T(1,128)} custom-call(f32[4,4,512,256]{3,2,1,0:T(8,128)} %get-tuple-element.6.x_ref), custom_call_target="tpu_custom_call" | custom-call | tf_op jit(solution)/shard_map/spread/pallas_call | solution.py:714

commit v4 on v3

--- a/solution.py
+++ b/solution.py
@@ -56,12 +56,18 @@
             src_ref=src, dst_ref=dst, send_sem=send, recv_sem=recv, device_id=device, device_id_type=MESH
         )
 
-    def send(copy, condition=None):
+    def go(copy, condition=None):
         if condition is None:
             copy.start()
         else:
             pl.when(condition)(copy.start)
-        pending.append((copy, condition))
+
+    def drain(sem, ref, condition=None):
+        pending.append((pltpu.make_async_copy(ref, ref, sem).wait, condition))
+
+    def send(copy, condition=None):
+        go(copy, condition)
+        pending.append((copy.wait_send, condition))
 
     def lanes(start, count):
         return pl.ds(pl.multiple_of(start, LANES), count)
@@ -102,7 +108,7 @@
     def plane_copy(mask, side, s, p, origin, source, device):
         m = member(s, p)
         dst = jr_ref.at[p, m, pl.ds(pl.multiple_of(origin * piece, piece), piece), :]
-        return remote(source if source is not None else dst, dst, jr_send.at[mask, side, s, p],
+        return remote(source if source is not None else dst, dst, jr_send.at[0],
                       jr_recv.at[mask, side, s, p], device)
 
     def plane_out(s, masks, pairs=range(pair_dev)):
@@ -112,7 +118,7 @@
                     if mask == 0 and side == 0:
                         continue
                     src = t_ref.at[p, :, part(member(s, p), layer)]
-                    send(plane_copy(mask, side, s, p, mine, src, (r, c ^ mask, layer)))
+                    go(plane_copy(mask, side, s, p, mine, src, (r, c ^ mask, layer)))
 
     seen = set()
 
@@ -128,7 +134,7 @@
     def plane_relay(s, p, mask):
         plane_wait(mask, s, p)
         for side, layer in ((0, l), (1, other)):
-            send(plane_copy(3, side, s, p, (c ^ mask) * 2 + layer, None, (r, c ^ mask ^ 3, l)))
+            go(plane_copy(3, side, s, p, (c ^ mask) * 2 + layer, None, (r, c ^ mask ^ 3, l)))
 
     same = r == c
     differs = r != c
@@ -142,13 +148,13 @@
 
     def handed(mask, s, p, src):
         return remote(
-            src, jo_ref.at[mask, s, p], jo_send.at[mask, s, p], jo_recv.at[mask, s, p], partner
+            src, jo_ref.at[mask, s, p], jo_send.at[0], jo_recv.at[mask, s, p], partner
         )
 
     def halves_out(s):
         for mask in range(cols_n):
             for p in range(pair_dev):
-                send(handed(mask, s, p, left_unit(mask, s, p)), same)
+                go(handed(mask, s, p, left_unit(mask, s, p)), same)
 
     kinds = (0, 1) if square else (0,)
 
@@ -171,11 +177,13 @@
             p = leading(r, k)
             for side, layer in ((0, l), (1, other)):
                 for up, there, to, _, recv in ways():
-                    send(remote(
+                    go(remote(
                         t_ref.at[p, :, part(member(s, p), layer)],
                         z_ref.at[r, 0, s, p, pl.ds(pl.multiple_of(l * piece, piece), piece), :],
-                        zo_send.at[int(up), side, s, p], recv.at[1, 0, s, p], (to, c, layer),
+                        zo_send.at[int(up), s], recv.at[1, 0, s, p], (to, c, layer),
                     ), there & carried(0, s, r, up))
+        for up, there, _, _, _ in ways():
+            drain(zo_send.at[int(up), s], z_ref.at[0, 0, s], there & carried(0, s, r, up))
 
     def rows_across(s, among=True):
         for p in range(pair_dev):
@@ -183,9 +191,11 @@
         for k in range(pair_dev):
             p = leading(r, k)
             for up, there, to, snd, recv in ways():
-                send(remote(
-                    left_unit(1, s, p), z_ref.at[r, 1, s, p], snd.at[0, 1, s, p], recv.at[1, 1, s, p], (to, c, l)
+                go(remote(
+                    left_unit(1, s, p), z_ref.at[r, 1, s, p], snd.at[0, 1, s], recv.at[1, 1, s, p], (to, c, l)
                 ), there & among & carried(1, s, r, up))
+        for up, there, _, snd, _ in ways():
+            drain(snd.at[0, 1, s], z_ref.at[0, 0, s], there & among & carried(1, s, r, up))
 
     def arrivals(s, step):
         for kind in kinds:
@@ -211,10 +221,12 @@
                     at_end = (at == 0) | (at == rows_n - 1)
                     chosen = chosen & (at_end if ends else jnp.logical_not(at_end))
                 mask = (c ^ at) ^ kind
-                send(remote(
-                    z_ref.at[at, kind, s, p], z_ref.at[at, mask, s, p], into.at[step, kind, s, p],
+                go(remote(
+                    z_ref.at[at, kind, s, p], z_ref.at[at, mask, s, p], into.at[step, kind, s],
                     jc_recv.at[mask, s, p], (r, at, l),
                 ), chosen)
+                if k + 1 == pair_dev:
+                    drain(into.at[step, kind, s], z_ref.at[0, 0, s], chosen)
 
     def forward(s, step, give=True, only=None, ends=None, clear=None):
         for k in range(pair_dev):
@@ -232,12 +244,14 @@
 
                 @pl.when(onward)
                 def _():
-                    remote(block_ref, block_ref, snd.at[step, kind, s, p], recv.at[step, kind, s, p],
+                    remote(block_ref, block_ref, snd.at[step, kind, s], recv.at[step, kind, s, p],
                            partner).wait_recv()
 
-                send(remote(
-                    block_ref, block_ref, snd.at[step, kind, s, p], recv.at[step + 1, kind, s, p], (to, c, l)
+                go(remote(
+                    block_ref, block_ref, snd.at[step, kind, s], recv.at[step + 1, kind, s, p], (to, c, l)
                 ), onward)
+                if k + 1 == pair_dev:
+                    drain(snd.at[step, kind, s], z_ref.at[0, 0, s], onward)
         if give:
             hand_over(s, step, True, only, ends)
 
@@ -249,7 +263,7 @@
 
                 @pl.when(here & jnp.logical_not(onward))
                 def _():
-                    remote(block_ref, block_ref, snd.at[step, kind, s, p], recv.at[step, kind, s, p],
+                    remote(block_ref, block_ref, snd.at[step, kind, s], recv.at[step, kind, s, p],
                            partner).wait_recv()
 
         hand_over(s, step, False, near=near)
@@ -335,7 +349,7 @@
             moved, target, at = has_next, r + 1, jnp.where(has_next, 0, 3)
         for n in order_of_tiles:
             src, dst = l_tile.at[(slot - 1) * width + n], lr_ref.at[at, n]
-            send(remote(src, dst, lr_send.at[slot, n], lr_recv.at[at, n], (target, c, l)), moved)
+            go(remote(src, dst, lr_send.at[slot - 1], lr_recv.at[at, n], (target, c, l)), moved)
             pl.when(jnp.logical_not(moved))(pltpu.make_async_copy(src, dst, lr_recv.at[at, n]).start)
 
     def right_pieces(s, p):
@@ -348,9 +362,9 @@
             if mask and not (square and mask == 1 and s == 1):
                 @pl.when(late)
                 def _():
-                    remote(unit, unit, jo_send.at[mask, s, p], jc_recv.at[mask, s, p], partner).wait_recv()
-
-            send(handed(mask, s, p, unit), differs)
+                    remote(unit, unit, jo_send.at[0], jc_recv.at[mask, s, p], partner).wait_recv()
+
+            go(handed(mask, s, p, unit), differs)
         jobs = [(side, mask) for side in range(2) for mask in range(cols_n)]
 
         def place(k):
@@ -426,12 +440,12 @@
             condition = moved if s == 0 else None
             if around is not None:
                 index = by_way.index(at)
-                send(remote(
-                    src, via_ref.at[index, l], o_send.at[tile, s], via_recv.at[index, l], (r, c ^ 2, layer)
+                go(remote(
+                    src, via_ref.at[index, l], o_send.at[0 if s else 1 + q], via_recv.at[index, l], (r, c ^ 2, layer)
                 ), around)
                 direct = jnp.logical_not(around)
                 condition = direct if condition is None else condition & direct
-            send(remote(src, dst, o_send.at[tile, s], o_recv.at[slot, l], (r, column, layer)), condition)
+            go(remote(src, dst, o_send.at[0 if s else 1 + q], o_recv.at[slot, l], (r, column, layer)), condition)
             if s == 0:
                 pl.when(jnp.logical_not(moved))(pltpu.make_async_copy(src, dst, o_recv.at[slot, l]).start)
 
@@ -439,8 +453,8 @@
         tile = right_tile(at, j, j // 2)
         slot = jnp.where(left_end, 2, 0) if j == 0 else 1
         dst = out_ref.at[slot, at, low_rows, :]
-        send(remote(
-            o_tile.at[tile, :, lanes(other * half, half)], dst, o_send.at[tile, 1], o_recv.at[slot, l], partner
+        go(remote(
+            o_tile.at[tile, :, lanes(other * half, half)], dst, o_send.at[0], o_recv.at[slot, l], partner
         ))
         pltpu.make_async_copy(
             o_tile.at[tile, :, lanes(l * half, half)], dst, o_recv.at[slot, l]
@@ -550,8 +564,7 @@
     with scope("turn_b"):
         turn(1)
     with scope("left_b"):
-        for slot in (width - 1, 0):
-            left(slot)
+        left(width - 1)
     if square:
         with scope("fwd_b1m"):
             forward(1, 1, only=1, ends=False)
@@ -559,18 +572,22 @@
     for tiles_first, tiles_last in ((first, last), (last, first)):
         left_out(width - 2, tiles_first)
         left_out(1, tiles_last)
-    with scope("rows"):
-        @pl.when(jnp.logical_not(has_prev))
-        def _():
-            for q in range(pair_dev):
-                left_rows(2, q)
     for k in range(pair_dev):
         q = leading(c, k)
         with scope("pieces_a"):
             right_pieces(0, q)
         with scope("right"):
-            for at in staying:
-                right_moving(at, q)
+            right_moving(staying[0], q)
+        if k == 0:
+            with scope("left_c"):
+                left(0)
+
+                @pl.when(jnp.logical_not(has_prev))
+                def _():
+                    for at in range(pair_dev):
+                        left_rows(2, at)
+        with scope("right"):
+            right_moving(staying[1], q)
 
     first, last = jnp.logical_not(has_prev), jnp.logical_not(has_next)
 
@@ -607,12 +624,19 @@
             for layer in range(2):
                 block_ref = out_ref.at[slot, :, pl.ds(layer * half, half), :]
                 pltpu.make_async_copy(block_ref, block_ref, o_recv.at[slot, layer]).wait()
+    drain(jr_send.at[0], jr_ref.at[:, :, pl.ds(0, (2 * cols_n - 1) * piece), :])
+    drain(jo_send.at[0], jo_ref)
+    drain(o_send.at[0], out_ref.at[pl.ds(0, width // 2)])
+    for q, moved in ((0, left_end), (1, right_end)):
+        drain(o_send.at[1 + q], out_ref.at[0, :, pl.ds(0, half), :], moved)
+    for slot, moved in ((1, has_prev), (width - 2, has_next)):
+        drain(lr_send.at[slot - 1], lr_ref.at[0], moved)
     with scope("send_wait"):
-        for copy, condition in pending:
+        for wait, condition in pending:
             if condition is None:
-                copy.wait_send()
+                wait()
             else:
-                pl.when(condition)(copy.wait_send)
+                pl.when(condition)(wait)
 
 
 def spread(size, x_ref, o_ref, buffer, in_sem, out_sem):
@@ -693,14 +717,14 @@
             vmem((2, half, block), f32),
             dma((2,)), dma((4 * pair_dev,)), dma((2,) + by_piece),
             dma((pair_dev,)), dma((pair_dev,)),
-            dma((cols_n, 2) + by_piece), dma((cols_n, 2) + by_piece),
-            dma((2, 2) + by_piece),
-            dma((rows_n, 2) + by_piece), dma((rows_n, 2) + by_piece),
-            dma((rows_n, 2) + by_piece), dma((rows_n, 2) + by_piece),
-            dma((rows_n, 2) + by_piece), dma((rows_n, 2) + by_piece), dma((cols_n,) + by_piece),
-            dma((cols_n,) + by_piece), dma((cols_n,) + by_piece),
-            dma((width, width)), dma((width, width)),
-            dma((width * width, 2)), dma((width, 2)),
+            dma((1,)), dma((cols_n, 2) + by_piece),
+            dma((2, 2)),
+            dma((rows_n, 2, 2)), dma((rows_n, 2) + by_piece),
+            dma((rows_n, 2, 2)), dma((rows_n, 2) + by_piece),
+            dma((rows_n, 2, 2)), dma((rows_n, 2, 2)), dma((cols_n,) + by_piece),
+            dma((1,)), dma((cols_n,) + by_piece),
+            dma((2,)), dma((width, width)),
+            dma((3,)), dma((width, 2)),
             dma((2, 2)), dma((2, 2)),
         ],
         compiler_params=pltpu.CompilerParams(

time: 154 us -> 152 us (0.987)
  Pallas kernels: 153 us -> 151 us
    pallas_call x1, Pallas kernels: 146 us -> 144 us  [shards(): pl.pallas_call(functools.partial(sweep, (rows_n, cols_n, pair_dev, width,...]
where the time goes in v4:
time: 152 us; the launch traced here: 151 us
  Pallas kernels  151 us (99%)
    pallas_call x1, Pallas kernels, shards(): pl.pallas_call(functools.partial(sweep, (rows_n, cols_n, pair_dev, width,...  144 us
    pallas_call x1, Pallas kernels, shards(): pl.pallas_call(functools.partial(spread, (width, block, tiles)), name='sp...  6.88 us

profile of v4, /device:TPU:5, one launch (start us, length us, event | category | flops | bytes accessed | tf_op | source)
XLA Modules:
  0.0 151.4 jit_solution(11256732144672647170)
XLA Ops:
  0.0 144.3 %sweep.1 = (f32[4,4,512,256]{3,2,1,0:T(8,128)}, f32[2048,8,1,128]{3,2,1,0:T(1,128)}, f32[2,2,1024,256]{3,2,1,0:T(8,128)}, f32[4,2,2,256,256]{4,3,2,1,0:T(8,128)}...) custom-call(f32[2048,8,1,128]{3,2,1,0:T(1,128)} %bitcast.11, ...), custom_call_target="tpu_custom_call" | custom-call | flops 25769803776 | tf_op jit(solution)/shard_map/sweep/pallas_call | solution.py:689
  144.3 6.9 %spread.1 = f32[2048,8,1,128]{3,2,1,0:T(1,128)} custom-call(f32[4,4,512,256]{3,2,1,0:T(8,128)} %get-tuple-element.6.x_ref), custom_call_target="tpu_custom_call" | custom-call | tf_op jit(solution)/shard_map/spread/pallas_call | solution.py:738
